TPU v7x, 8 devices: a whole 2x2x1 slice. The times are simulated.
8 devices in a mesh: data: 2 (over z, y), stage: 4 (over x, core).
Axes of the slice: x: 2, y: 2, z: 1, core: 2. Of those that a mesh axis runs over, the one named last changes fastest.
Arguments:
- X: bfloat16 [8, 1024, 2048], P('data'), parts along dimension 0
- G: bfloat16 [8, 1024, 2048], P('data'), parts along dimension 0
- W1: bfloat16 [4, 2048, 8192], P('stage')
- W2: bfloat16 [4, 8192, 2048], P('stage')
Outputs:
- output 1: bfloat16 [8, 1024, 2048], P('data'), parts along dimension 0
- output 2: bfloat16 [8, 1024, 2048], P('data'), parts along dimension 0
- output 3: float32 [8, 2048, 8192], P(('data', 'stage')), parts along dimension 0
- output 4: float32 [8, 8192, 2048], P(('data', 'stage')), parts along dimension 0
There are 2 independent parts. A program takes and returns all parts, laid end to end along the dimension named above; an argument that names none is the same for every part.
All inputs are finite; a program needn't handle non-finite values.
Results may differ from a plain program's by a relative error of at most 0.00996297.
Values are sent between devices in bfloat16 or wider.
A program may use at most 1 GiB of HBM per device.

v0:
```python
import jax
import jax.numpy as jnp
from jax import lax
from jax.sharding import PartitionSpec as P


def _fwd_layer(h, w1, w2):
    z = jnp.dot(h, w1, preferred_element_type=jnp.float32)
    u = jax.nn.gelu(z, approximate=True).astype(jnp.bfloat16)
    return (h.astype(jnp.float32) + jnp.dot(u, w2, preferred_element_type=jnp.float32)).astype(jnp.bfloat16)


def _bwd_layer(h, g, w1, w2):
    z = jnp.dot(h, w1, preferred_element_type=jnp.float32)
    u, gelu_vjp = jax.vjp(lambda t: jax.nn.gelu(t, approximate=True), z)
    du = jnp.dot(g, w2.T, preferred_element_type=jnp.float32)
    dz = gelu_vjp(du)[0].astype(jnp.bfloat16)
    dw2 = jnp.dot(u.astype(jnp.bfloat16).T, g, preferred_element_type=jnp.float32)
    dw1 = jnp.dot(h.T, dz, preferred_element_type=jnp.float32)
    dh = (g.astype(jnp.float32) + jnp.dot(dz, w1.T, preferred_element_type=jnp.float32)).astype(jnp.bfloat16)
    return dh, dw1, dw2


def _put(buf, i, val, ok):
    old = lax.dynamic_index_in_dim(buf, i, 0, keepdims=False)
    return lax.dynamic_update_index_in_dim(buf, jnp.where(ok, val, old), i, 0)


def solution(mesh):
    n_st = mesh.shape['stage']
    fwd_perm = [(i, i + 1) for i in range(n_st - 1)]
    bwd_perm = [(i + 1, i) for i in range(n_st - 1)]

    def body(x, g, w1, w2):
        s = lax.axis_index('stage')
        n_mb = x.shape[0]
        lps = w1.shape[0]
        first = s == 0
        last = s == n_st - 1
        ticks = n_mb + n_st - 1
        mb_shape = x.shape[1:]

        def fwd_tick(t, carry):
            recv, saved, y = carry
            m = t - s
            ok = (m >= 0) & (m < n_mb)
            mc = jnp.clip(m, 0, n_mb - 1)
            h = jnp.where(first, lax.dynamic_index_in_dim(x, mc, 0, keepdims=False), recv)
            hs = []
            for j in range(lps):
                hs.append(h)
                h = _fwd_layer(h, w1[j], w2[j])
            saved = _put(saved, mc, jnp.stack(hs), ok)
            y = _put(y, mc, h, ok & last)
            recv = lax.ppermute(h, 'stage', fwd_perm)
            return recv, saved, y

        recv0 = jnp.zeros(mb_shape, x.dtype)
        saved0 = jnp.zeros((n_mb, lps) + mb_shape, x.dtype)
        _, saved, y = lax.fori_loop(0, ticks, fwd_tick, (recv0, saved0, jnp.zeros_like(x)))

        def bwd_tick(t, carry):
            recv, dx, a1, a2 = carry
            m = t - (n_st - 1 - s)
            ok = (m >= 0) & (m < n_mb)
            mc = jnp.clip(m, 0, n_mb - 1)
            gh = jnp.where(last, lax.dynamic_index_in_dim(g, mc, 0, keepdims=False), recv)
            hs = lax.dynamic_index_in_dim(saved, mc, 0, keepdims=False)
            a1 = list(a1)
            a2 = list(a2)
            for j in reversed(range(lps)):
                gh, dw1, dw2 = _bwd_layer(hs[j], gh, w1[j], w2[j])
                a1[j] = a1[j] + jnp.where(ok, dw1, 0.0)
                a2[j] = a2[j] + jnp.where(ok, dw2, 0.0)
            dx = _put(dx, mc, gh, ok & first)
            recv = lax.ppermute(gh, 'stage', bwd_perm)
            return recv, dx, tuple(a1), tuple(a2)

        a10 = tuple(jnp.zeros(w1.shape[1:], jnp.float32) for _ in range(lps))
        a20 = tuple(jnp.zeros(w2.shape[1:], jnp.float32) for _ in range(lps))
        _, dx, a1, a2 = lax.fori_loop(0, ticks, bwd_tick, (recv0, jnp.zeros_like(x), a10, a20))
        y = lax.psum(y, 'stage')
        dx = lax.psum(dx, 'stage')
        return y, dx, jnp.stack(a1), jnp.stack(a2)

    return jax.shard_map(body, mesh=mesh,
                         in_specs=(P('data'), P('data'), P('stage'), P('stage')),
                         out_specs=(P('data'), P('data'), P(('data', 'stage')), P(('data', 'stage'))),
                         check_vma=False)
```

profile of v0, /device:TPU:7, one launch (start us, length us, event | category | flops | bytes accessed | tf_op | source)
XLA Modules:
  0.0 3718.7 jit_solution(11523678943093489518)
XLA Ops:
  21.9 1035.9 %while.39 = (s32[]{:T(128)}, bf16[1024,2048]{1,0:T(8,128)(2,1)}, bf16[4,1,1024,2048]{3,2,1,0:T(8,128)(2,1)}, bf16[4,1024,2048]{2,1,0:T(8,128)(2,1)}, pred[]{:T(5...) while((s32[]{:T(128)}, bf16[1024,2048]{1,0:T(8,128)(2,1)}, ...), condition=%wide.region_1.2_spmd, body=%wide.region_0.1_spmd.sunk | while | flops 68811751424 | bytes 188745472 | solution.py:60
  26.7 48.1 %fusion.25.clone.6 = bf16[1024,8192]{1,0:T(8,128)(2,1)} fusion(bf16[1,2048,8192]{2,1,0:T(8,128)(2,1)} %get-tuple-element.735, bf16[1024,2048]{1,0:T(8,128)(2,1)} %get-tuple-element.715, bf16[4,1024,2048]{2,1,0:T(8,128)(2,1)} %get-tuple-element.734, s32[]{:T(128)S(6)} %min.21, pred[]{:T(512)} %get-tuple-element.732), kind=kOutput, calls=%fused_computation.8.clone.clone.clone.clone.clone.clone.1.clone.1 | convolution fusion | flops 34437332992 | bytes 58720772 | tf_op jit(solution)/shard_map/while/body/eval_jaxpr/dot_general | solution.py:8
  142.9 48.1 %fusion.25.clone.6 = bf16[1024,8192]{1,0:T(8,128)(2,1)} fusion(bf16[1,2048,8192]{2,1,0:T(8,128)(2,1)} %get-tuple-element.735, bf16[1024,2048]{1,0:T(8,128)(2,1)} %get-tuple-element.715, bf16[4,1024,2048]{2,1,0:T(8,128)(2,1)} %get-tuple-element.734, s32[]{:T(128)S(6)} %min.21, pred[]{:T(512)} %get-tuple-element.732), kind=kOutput, calls=%fused_computation.8.clone.clone.clone.clone.clone.clone.1.clone.1 | convolution fusion | flops 34437332992 | bytes 58720772 | tf_op jit(solution)/shard_map/while/body/eval_jaxpr/dot_general | solution.py:8
  293.6 48.1 %fusion.25.clone.6 = bf16[1024,8192]{1,0:T(8,128)(2,1)} fusion(bf16[1,2048,8192]{2,1,0:T(8,128)(2,1)} %get-tuple-element.735, bf16[1024,2048]{1,0:T(8,128)(2,1)} %get-tuple-element.715, bf16[4,1024,2048]{2,1,0:T(8,128)(2,1)} %get-tuple-element.734, s32[]{:T(128)S(6)} %min.21, pred[]{:T(512)} %get-tuple-element.732), kind=kOutput, calls=%fused_computation.8.clone.clone.clone.clone.clone.clone.1.clone.1 | convolution fusion | flops 34437332992 | bytes 58720772 | tf_op jit(solution)/shard_map/while/body/eval_jaxpr/dot_general | solution.py:8
  447.4 48.1 %fusion.25.clone.6 = bf16[1024,8192]{1,0:T(8,128)(2,1)} fusion(bf16[1,2048,8192]{2,1,0:T(8,128)(2,1)} %get-tuple-element.735, bf16[1024,2048]{1,0:T(8,128)(2,1)} %get-tuple-element.715, bf16[4,1024,2048]{2,1,0:T(8,128)(2,1)} %get-tuple-element.734, s32[]{:T(128)S(6)} %min.21, pred[]{:T(512)} %get-tuple-element.732), kind=kOutput, calls=%fused_computation.8.clone.clone.clone.clone.clone.clone.1.clone.1 | convolution fusion | flops 34437332992 | bytes 58720772 | tf_op jit(solution)/shard_map/while/body/eval_jaxpr/dot_general | solution.py:8
  601.2 48.1 %fusion.25.clone.6 = bf16[1024,8192]{1,0:T(8,128)(2,1)} fusion(bf16[1,2048,8192]{2,1,0:T(8,128)(2,1)} %get-tuple-element.735, bf16[1024,2048]{1,0:T(8,128)(2,1)} %get-tuple-element.715, bf16[4,1024,2048]{2,1,0:T(8,128)(2,1)} %get-tuple-element.734, s32[]{:T(128)S(6)} %min.21, pred[]{:T(512)} %get-tuple-element.732), kind=kOutput, calls=%fused_computation.8.clone.clone.clone.clone.clone.clone.1.clone.1 | convolution fusion | flops 34437332992 | bytes 58720772 | tf_op jit(solution)/shard_map/while/body/eval_jaxpr/dot_general | solution.py:8
  755.0 48.1 %fusion.25.clone.6 = bf16[1024,8192]{1,0:T(8,128)(2,1)} fusion(bf16[1,2048,8192]{2,1,0:T(8,128)(2,1)} %get-tuple-element.735, bf16[1024,2048]{1,0:T(8,128)(2,1)} %get-tuple-element.715, bf16[4,1024,2048]{2,1,0:T(8,128)(2,1)} %get-tuple-element.734, s32[]{:T(128)S(6)} %min.21, pred[]{:T(512)} %get-tuple-element.732), kind=kOutput, calls=%fused_computation.8.clone.clone.clone.clone.clone.clone.1.clone.1 | convolution fusion | flops 34437332992 | bytes 58720772 | tf_op jit(solution)/shard_map/while/body/eval_jaxpr/dot_general | solution.py:8
  908.8 48.1 %fusion.25.clone.6 = bf16[1024,8192]{1,0:T(8,128)(2,1)} fusion(bf16[1,2048,8192]{2,1,0:T(8,128)(2,1)} %get-tuple-element.735, bf16[1024,2048]{1,0:T(8,128)(2,1)} %get-tuple-element.715, bf16[4,1024,2048]{2,1,0:T(8,128)(2,1)} %get-tuple-element.734, s32[]{:T(128)S(6)} %min.21, pred[]{:T(512)} %get-tuple-element.732), kind=kOutput, calls=%fused_computation.8.clone.clone.clone.clone.clone.clone.1.clone.1 | convolution fusion | flops 34437332992 | bytes 58720772 | tf_op jit(solution)/shard_map/while/body/eval_jaxpr/dot_general | solution.py:8
  1066.3 2070.0 %while.40 = (s32[]{:T(128)}, bf16[1024,2048]{1,0:T(8,128)(2,1)}, bf16[4,1024,2048]{2,1,0:T(8,128)(2,1)}, f32[2048,8192]{1,0:T(8,128)}, f32[8192,2048]{1,0:T(8,12...) while((s32[]{:T(128)}, bf16[1024,2048]{1,0:T(8,128)(2,1)}, ...), condition=%wide.region_4.5_spmd.clone, body=%wide.region_3.4_spmd.clone.sunk | while | flops 172153110528 | bytes 591397120 | solution.py:81
  1136.3 62.5 %fusion.100 = bf16[1024,8192]{1,0:T(8,128)(2,1)} fusion(f32[1024,8192]{1,0:T(8,128)} %fusion.99, bf16[1024,2048]{1,0:T(8,128)(2,1)} %bitcast_select_fusion.15, bf16[1,8192,2048]{2,1,0:T(8,128)(2,1)} %get-tuple-element.782), kind=kOutput, calls=%fused_computation.39.clone.1 | convolution fusion | flops 34527510528 | bytes 88080384 | tf_op jit(solution)/shard_map/while/body/eval_jaxpr/dot_general | solution.py:16
  1243.9 46.5 %collective-permute-start.1 = (bf16[1024,2048]{1,0:T(8,128)(2,1)}, bf16[1024,2048]{1,0:T(8,128)(2,1)}, u32[]{:S(2)}, u32[]{:S(2)}) collective-permute-start(bf16[1024,2048]{1,0:T(8,128)(2,1)} %get-tuple-element.698), channel_id=1, source_target_pairs={{1,0},{2,1},{3,2},{5,4},{6,5},{7,6}} | collective-permute-start | bytes 12582920 | tf_op jit(solution)/shard_map/while/body/eval_jaxpr/ppermute | solution.py:76
  1290.4 48.5 %select_add_fusion.4 = f32[2048,8192]{1,0:T(8,128)} fusion(f32[2048,8192]{1,0:T(8,128)} %get-tuple-element.761, bf16[1024,8192]{1,0:T(8,128)(2,1)} %fusion.100, pred[]{:T(512)S(6)} %compare.3, pred[]{:T(512)S(6)} %and.43, bf16[4,1,1024,2048]{3,2,1,0:T(8,128)(2,1)} %get-tuple-element.783, s32[]{:T(128)S(6)} %min.22), kind=kOutput, calls=%fused_computation.30.clone.2 | convolution fusion | flops 34410070016 | bytes 155189248 | tf_op jit(solution)/shard_map/while/body/eval_jaxpr/dot_general | solution.py:19
  1338.8 48.0 %select_add_fusion.5 = f32[8192,2048]{1,0:T(8,128)} fusion(f32[8192,2048]{1,0:T(8,128)} %get-tuple-element.762, bf16[1024,2048]{1,0:T(8,128)(2,1)} %bitcast_select_fusion.15, pred[]{:T(512)S(6)} %compare.3, pred[]{:T(512)S(6)} %and.43, f32[1024,8192]{1,0:T(8,128)} %fusion.99), kind=kOutput, calls=%fused_computation.29.clone.2 | convolution fusion | flops 34485567488 | bytes 171966464 | tf_op jit(solution)/shard_map/while/body/eval_jaxpr/dot_general | solution.py:18
  1437.7 62.5 %fusion.100 = bf16[1024,8192]{1,0:T(8,128)(2,1)} fusion(f32[1024,8192]{1,0:T(8,128)} %fusion.99, bf16[1024,2048]{1,0:T(8,128)(2,1)} %bitcast_select_fusion.15, bf16[1,8192,2048]{2,1,0:T(8,128)(2,1)} %get-tuple-element.782), kind=kOutput, calls=%fused_computation.39.clone.1 | convolution fusion | flops 34527510528 | bytes 88080384 | tf_op jit(solution)/shard_map/while/body/eval_jaxpr/dot_general | solution.py:16
  1548.4 63.2 %select_add_fusion.4 = f32[2048,8192]{1,0:T(8,128)} fusion(f32[2048,8192]{1,0:T(8,128)} %get-tuple-element.761, bf16[1024,8192]{1,0:T(8,128)(2,1)} %fusion.100, pred[]{:T(512)S(6)} %compare.3, pred[]{:T(512)S(6)} %and.43, bf16[4,1,1024,2048]{3,2,1,0:T(8,128)(2,1)} %get-tuple-element.783, s32[]{:T(128)S(6)} %min.22), kind=kOutput, calls=%fused_computation.30.clone.2 | convolution fusion | flops 34410070016 | bytes 155189248 | tf_op jit(solution)/shard_map/while/body/eval_jaxpr/dot_general | solution.py:19
  1611.6 66.9 %select_add_fusion.5 = f32[8192,2048]{1,0:T(8,128)} fusion(f32[8192,2048]{1,0:T(8,128)} %get-tuple-element.762, bf16[1024,2048]{1,0:T(8,128)(2,1)} %bitcast_select_fusion.15, pred[]{:T(512)S(6)} %compare.3, pred[]{:T(512)S(6)} %and.43, f32[1024,8192]{1,0:T(8,128)} %fusion.99), kind=kOutput, calls=%fused_computation.29.clone.2 | convolution fusion | flops 34485567488 | bytes 171966464 | tf_op jit(solution)/shard_map/while/body/eval_jaxpr/dot_general | solution.py:18
  1729.3 62.5 %fusion.100 = bf16[1024,8192]{1,0:T(8,128)(2,1)} fusion(f32[1024,8192]{1,0:T(8,128)} %fusion.99, bf16[1024,2048]{1,0:T(8,128)(2,1)} %bitcast_select_fusion.15, bf16[1,8192,2048]{2,1,0:T(8,128)(2,1)} %get-tuple-element.782), kind=kOutput, calls=%fused_computation.39.clone.1 | convolution fusion | flops 34527510528 | bytes 88080384 | tf_op jit(solution)/shard_map/while/body/eval_jaxpr/dot_general | solution.py:16
  1840.0 63.2 %select_add_fusion.4 = f32[2048,8192]{1,0:T(8,128)} fusion(f32[2048,8192]{1,0:T(8,128)} %get-tuple-element.761, bf16[1024,8192]{1,0:T(8,128)(2,1)} %fusion.100, pred[]{:T(512)S(6)} %compare.3, pred[]{:T(512)S(6)} %and.43, bf16[4,1,1024,2048]{3,2,1,0:T(8,128)(2,1)} %get-tuple-element.783, s32[]{:T(128)S(6)} %min.22), kind=kOutput, calls=%fused_computation.30.clone.2 | convolution fusion | flops 34410070016 | bytes 155189248 | tf_op jit(solution)/shard_map/while/body/eval_jaxpr/dot_general | solution.py:19
  1903.2 66.9 %select_add_fusion.5 = f32[8192,2048]{1,0:T(8,128)} fusion(f32[8192,2048]{1,0:T(8,128)} %get-tuple-element.762, bf16[1024,2048]{1,0:T(8,128)(2,1)} %bitcast_select_fusion.15, pred[]{:T(512)S(6)} %compare.3, pred[]{:T(512)S(6)} %and.43, f32[1024,8192]{1,0:T(8,128)} %fusion.99), kind=kOutput, calls=%fused_computation.29.clone.2 | convolution fusion | flops 34485567488 | bytes 171966464 | tf_op jit(solution)/shard_map/while/body/eval_jaxpr/dot_general | solution.py:18
  2020.9 62.5 %fusion.100 = bf16[1024,8192]{1,0:T(8,128)(2,1)} fusion(f32[1024,8192]{1,0:T(8,128)} %fusion.99, bf16[1024,2048]{1,0:T(8,128)(2,1)} %bitcast_select_fusion.15, bf16[1,8192,2048]{2,1,0:T(8,128)(2,1)} %get-tuple-element.782), kind=kOutput, calls=%fused_computation.39.clone.1 | convolution fusion | flops 34527510528 | bytes 88080384 | tf_op jit(solution)/shard_map/while/body/eval_jaxpr/dot_general | solution.py:16
  2131.6 63.2 %select_add_fusion.4 = f32[2048,8192]{1,0:T(8,128)} fusion(f32[2048,8192]{1,0:T(8,128)} %get-tuple-element.761, bf16[1024,8192]{1,0:T(8,128)(2,1)} %fusion.100, pred[]{:T(512)S(6)} %compare.3, pred[]{:T(512)S(6)} %and.43, bf16[4,1,1024,2048]{3,2,1,0:T(8,128)(2,1)} %get-tuple-element.783, s32[]{:T(128)S(6)} %min.22), kind=kOutput, calls=%fused_computation.30.clone.2 | convolution fusion | flops 34410070016 | bytes 155189248 | tf_op jit(solution)/shard_map/while/body/eval_jaxpr/dot_general | solution.py:19
  2194.8 66.9 %select_add_fusion.5 = f32[8192,2048]{1,0:T(8,128)} fusion(f32[8192,2048]{1,0:T(8,128)} %get-tuple-element.762, bf16[1024,2048]{1,0:T(8,128)(2,1)} %bitcast_select_fusion.15, pred[]{:T(512)S(6)} %compare.3, pred[]{:T(512)S(6)} %and.43, f32[1024,8192]{1,0:T(8,128)} %fusion.99), kind=kOutput, calls=%fused_computation.29.clone.2 | convolution fusion | flops 34485567488 | bytes 171966464 | tf_op jit(solution)/shard_map/while/body/eval_jaxpr/dot_general | solution.py:18
  2312.4 62.5 %fusion.100 = bf16[1024,8192]{1,0:T(8,128)(2,1)} fusion(f32[1024,8192]{1,0:T(8,128)} %fusion.99, bf16[1024,2048]{1,0:T(8,128)(2,1)} %bitcast_select_fusion.15, bf16[1,8192,2048]{2,1,0:T(8,128)(2,1)} %get-tuple-element.782), kind=kOutput, calls=%fused_computation.39.clone.1 | convolution fusion | flops 34527510528 | bytes 88080384 | tf_op jit(solution)/shard_map/while/body/eval_jaxpr/dot_general | solution.py:16
  2423.2 63.2 %select_add_fusion.4 = f32[2048,8192]{1,0:T(8,128)} fusion(f32[2048,8192]{1,0:T(8,128)} %get-tuple-element.761, bf16[1024,8192]{1,0:T(8,128)(2,1)} %fusion.100, pred[]{:T(512)S(6)} %compare.3, pred[]{:T(512)S(6)} %and.43, bf16[4,1,1024,2048]{3,2,1,0:T(8,128)(2,1)} %get-tuple-element.783, s32[]{:T(128)S(6)} %min.22), kind=kOutput, calls=%fused_computation.30.clone.2 | convolution fusion | flops 34410070016 | bytes 155189248 | tf_op jit(solution)/shard_map/while/body/eval_jaxpr/dot_general | solution.py:19
  2486.3 66.9 %select_add_fusion.5 = f32[8192,2048]{1,0:T(8,128)} fusion(f32[8192,2048]{1,0:T(8,128)} %get-tuple-element.762, bf16[1024,2048]{1,0:T(8,128)(2,1)} %bitcast_select_fusion.15, pred[]{:T(512)S(6)} %compare.3, pred[]{:T(512)S(6)} %and.43, f32[1024,8192]{1,0:T(8,128)} %fusion.99), kind=kOutput, calls=%fused_computation.29.clone.2 | convolution fusion | flops 34485567488 | bytes 171966464 | tf_op jit(solution)/shard_map/while/body/eval_jaxpr/dot_general | solution.py:18
  2604.0 62.5 %fusion.100 = bf16[1024,8192]{1,0:T(8,128)(2,1)} fusion(f32[1024,8192]{1,0:T(8,128)} %fusion.99, bf16[1024,2048]{1,0:T(8,128)(2,1)} %bitcast_select_fusion.15, bf16[1,8192,2048]{2,1,0:T(8,128)(2,1)} %get-tuple-element.782), kind=kOutput, calls=%fused_computation.39.clone.1 | convolution fusion | flops 34527510528 | bytes 88080384 | tf_op jit(solution)/shard_map/while/body/eval_jaxpr/dot_general | solution.py:16
  2714.7 63.2 %select_add_fusion.4 = f32[2048,8192]{1,0:T(8,128)} fusion(f32[2048,8192]{1,0:T(8,128)} %get-tuple-element.761, bf16[1024,8192]{1,0:T(8,128)(2,1)} %fusion.100, pred[]{:T(512)S(6)} %compare.3, pred[]{:T(512)S(6)} %and.43, bf16[4,1,1024,2048]{3,2,1,0:T(8,128)(2,1)} %get-tuple-element.783, s32[]{:T(128)S(6)} %min.22), kind=kOutput, calls=%fused_computation.30.clone.2 | convolution fusion | flops 34410070016 | bytes 155189248 | tf_op jit(solution)/shard_map/while/body/eval_jaxpr/dot_general | solution.py:19
  2777.9 66.9 %select_add_fusion.5 = f32[8192,2048]{1,0:T(8,128)} fusion(f32[8192,2048]{1,0:T(8,128)} %get-tuple-element.762, bf16[1024,2048]{1,0:T(8,128)(2,1)} %bitcast_select_fusion.15, pred[]{:T(512)S(6)} %compare.3, pred[]{:T(512)S(6)} %and.43, f32[1024,8192]{1,0:T(8,128)} %fusion.99), kind=kOutput, calls=%fused_computation.29.clone.2 | convolution fusion | flops 34485567488 | bytes 171966464 | tf_op jit(solution)/shard_map/while/body/eval_jaxpr/dot_general | solution.py:18
  2895.5 62.5 %fusion.100 = bf16[1024,8192]{1,0:T(8,128)(2,1)} fusion(f32[1024,8192]{1,0:T(8,128)} %fusion.99, bf16[1024,2048]{1,0:T(8,128)(2,1)} %bitcast_select_fusion.15, bf16[1,8192,2048]{2,1,0:T(8,128)(2,1)} %get-tuple-element.782), kind=kOutput, calls=%fused_computation.39.clone.1 | convolution fusion | flops 34527510528 | bytes 88080384 | tf_op jit(solution)/shard_map/while/body/eval_jaxpr/dot_general | solution.py:16
  3006.3 63.2 %select_add_fusion.4 = f32[2048,8192]{1,0:T(8,128)} fusion(f32[2048,8192]{1,0:T(8,128)} %get-tuple-element.761, bf16[1024,8192]{1,0:T(8,128)(2,1)} %fusion.100, pred[]{:T(512)S(6)} %compare.3, pred[]{:T(512)S(6)} %and.43, bf16[4,1,1024,2048]{3,2,1,0:T(8,128)(2,1)} %get-tuple-element.783, s32[]{:T(128)S(6)} %min.22), kind=kOutput, calls=%fused_computation.30.clone.2 | convolution fusion | flops 34410070016 | bytes 155189248 | tf_op jit(solution)/shard_map/while/body/eval_jaxpr/dot_general | solution.py:19
  3069.4 66.9 %select_add_fusion.5 = f32[8192,2048]{1,0:T(8,128)} fusion(f32[8192,2048]{1,0:T(8,128)} %get-tuple-element.762, bf16[1024,2048]{1,0:T(8,128)(2,1)} %bitcast_select_fusion.15, pred[]{:T(512)S(6)} %compare.3, pred[]{:T(512)S(6)} %and.43, f32[1024,8192]{1,0:T(8,128)} %fusion.99), kind=kOutput, calls=%fused_computation.29.clone.2 | convolution fusion | flops 34485567488 | bytes 171966464 | tf_op jit(solution)/shard_map/while/body/eval_jaxpr/dot_general | solution.py:18
  3136.3 552.1 %all-reduce.3.cloned.1.call-done = (bf16[4,1024,2048]{2,1,0:T(8,128)(2,1)}, bf16[4,1024,2048]{2,1,0:T(8,128)(2,1)}) async-done(((bf16[4,1024,2048]{2,1,0:T(8,128)(2,1)}, bf16[4,1024,2048]{2,1,0:T(8,128)(2,1)}), (bf16[4,1024,2048]{2,1,0:T(8,128)(2,1)}, bf16[4,1024,2048]{2,1,0:T(8,128)(2,1)})) %all-reduce.3.cloned.1.call-update) | async-done | bytes 33554448 | tf_op jit(solution)/shard_map/psum | solution.py:82
  (103 shorter events, 1434.9 us)
Async XLA Ops:
  7.2 3681.3 %all-reduce.3.cloned.1.call-start = ((), (), s32[]{:S(2)}) async-start(), calls=%async_computation | async-start | bytes 67108864 | tf_op jit(solution)/shard_map/psum | solution.py:82
  121.2 12.2 collective-permute-start
  237.4 46.8 %collective-permute-start = (bf16[1024,2048]{1,0:T(8,128)(2,1)}, bf16[1024,2048]{1,0:T(8,128)(2,1)}, u32[]{:S(2)}, u32[]{:S(2)}) collective-permute-start(bf16[1024,2048]{1,0:T(8,128)(2,1)} %get-tuple-element.684), channel_id=1, source_target_pairs={{0,1},{1,2},{2,3},{4,5},{5,6},{6,7}} | collective-permute-start | bytes 12582920 | tf_op jit(solution)/shard_map/while/body/eval_jaxpr/ppermute | solution.py:55
  388.1 49.8 %collective-permute-start = (bf16[1024,2048]{1,0:T(8,128)(2,1)}, bf16[1024,2048]{1,0:T(8,128)(2,1)}, u32[]{:S(2)}, u32[]{:S(2)}) collective-permute-start(bf16[1024,2048]{1,0:T(8,128)(2,1)} %get-tuple-element.684), channel_id=1, source_target_pairs={{0,1},{1,2},{2,3},{4,5},{5,6},{6,7}} | collective-permute-start | bytes 12582920 | tf_op jit(solution)/shard_map/while/body/eval_jaxpr/ppermute | solution.py:55
  541.9 49.8 %collective-permute-start = (bf16[1024,2048]{1,0:T(8,128)(2,1)}, bf16[1024,2048]{1,0:T(8,128)(2,1)}, u32[]{:S(2)}, u32[]{:S(2)}) collective-permute-start(bf16[1024,2048]{1,0:T(8,128)(2,1)} %get-tuple-element.684), channel_id=1, source_target_pairs={{0,1},{1,2},{2,3},{4,5},{5,6},{6,7}} | collective-permute-start | bytes 12582920 | tf_op jit(solution)/shard_map/while/body/eval_jaxpr/ppermute | solution.py:55
  695.7 49.8 %collective-permute-start = (bf16[1024,2048]{1,0:T(8,128)(2,1)}, bf16[1024,2048]{1,0:T(8,128)(2,1)}, u32[]{:S(2)}, u32[]{:S(2)}) collective-permute-start(bf16[1024,2048]{1,0:T(8,128)(2,1)} %get-tuple-element.684), channel_id=1, source_target_pairs={{0,1},{1,2},{2,3},{4,5},{5,6},{6,7}} | collective-permute-start | bytes 12582920 | tf_op jit(solution)/shard_map/while/body/eval_jaxpr/ppermute | solution.py:55
  849.5 49.8 %collective-permute-start = (bf16[1024,2048]{1,0:T(8,128)(2,1)}, bf16[1024,2048]{1,0:T(8,128)(2,1)}, u32[]{:S(2)}, u32[]{:S(2)}) collective-permute-start(bf16[1024,2048]{1,0:T(8,128)(2,1)} %get-tuple-element.684), channel_id=1, source_target_pairs={{0,1},{1,2},{2,3},{4,5},{5,6},{6,7}} | collective-permute-start | bytes 12582920 | tf_op jit(solution)/shard_map/while/body/eval_jaxpr/ppermute | solution.py:55
  1003.3 49.8 %collective-permute-start = (bf16[1024,2048]{1,0:T(8,128)(2,1)}, bf16[1024,2048]{1,0:T(8,128)(2,1)}, u32[]{:S(2)}, u32[]{:S(2)}) collective-permute-start(bf16[1024,2048]{1,0:T(8,128)(2,1)} %get-tuple-element.684), channel_id=1, source_target_pairs={{0,1},{1,2},{2,3},{4,5},{5,6},{6,7}} | collective-permute-start | bytes 12582920 | tf_op jit(solution)/shard_map/while/body/eval_jaxpr/ppermute | solution.py:55
  1243.9 143.0 %collective-permute-start.1 = (bf16[1024,2048]{1,0:T(8,128)(2,1)}, bf16[1024,2048]{1,0:T(8,128)(2,1)}, u32[]{:S(2)}, u32[]{:S(2)}) collective-permute-start(bf16[1024,2048]{1,0:T(8,128)(2,1)} %get-tuple-element.698), channel_id=1, source_target_pairs={{1,0},{2,1},{3,2},{5,4},{6,5},{7,6}} | collective-permute-start | bytes 12582920 | tf_op jit(solution)/shard_map/while/body/eval_jaxpr/ppermute | solution.py:76
  1545.2 133.3 %collective-permute-start.1 = (bf16[1024,2048]{1,0:T(8,128)(2,1)}, bf16[1024,2048]{1,0:T(8,128)(2,1)}, u32[]{:S(2)}, u32[]{:S(2)}) collective-permute-start(bf16[1024,2048]{1,0:T(8,128)(2,1)} %get-tuple-element.698), channel_id=1, source_target_pairs={{1,0},{2,1},{3,2},{5,4},{6,5},{7,6}} | collective-permute-start | bytes 12582920 | tf_op jit(solution)/shard_map/while/body/eval_jaxpr/ppermute | solution.py:76
  1836.7 133.4 %collective-permute-start.1 = (bf16[1024,2048]{1,0:T(8,128)(2,1)}, bf16[1024,2048]{1,0:T(8,128)(2,1)}, u32[]{:S(2)}, u32[]{:S(2)}) collective-permute-start(bf16[1024,2048]{1,0:T(8,128)(2,1)} %get-tuple-element.698), channel_id=1, source_target_pairs={{1,0},{2,1},{3,2},{5,4},{6,5},{7,6}} | collective-permute-start | bytes 12582920 | tf_op jit(solution)/shard_map/while/body/eval_jaxpr/ppermute | solution.py:76
  2128.3 133.3 %collective-permute-start.1 = (bf16[1024,2048]{1,0:T(8,128)(2,1)}, bf16[1024,2048]{1,0:T(8,128)(2,1)}, u32[]{:S(2)}, u32[]{:S(2)}) collective-permute-start(bf16[1024,2048]{1,0:T(8,128)(2,1)} %get-tuple-element.698), channel_id=1, source_target_pairs={{1,0},{2,1},{3,2},{5,4},{6,5},{7,6}} | collective-permute-start | bytes 12582920 | tf_op jit(solution)/shard_map/while/body/eval_jaxpr/ppermute | solution.py:76
  2419.9 133.3 %collective-permute-start.1 = (bf16[1024,2048]{1,0:T(8,128)(2,1)}, bf16[1024,2048]{1,0:T(8,128)(2,1)}, u32[]{:S(2)}, u32[]{:S(2)}) collective-permute-start(bf16[1024,2048]{1,0:T(8,128)(2,1)} %get-tuple-element.698), channel_id=1, source_target_pairs={{1,0},{2,1},{3,2},{5,4},{6,5},{7,6}} | collective-permute-start | bytes 12582920 | tf_op jit(solution)/shard_map/while/body/eval_jaxpr/ppermute | solution.py:76
  2711.5 133.3 %collective-permute-start.1 = (bf16[1024,2048]{1,0:T(8,128)(2,1)}, bf16[1024,2048]{1,0:T(8,128)(2,1)}, u32[]{:S(2)}, u32[]{:S(2)}) collective-permute-start(bf16[1024,2048]{1,0:T(8,128)(2,1)} %get-tuple-element.698), channel_id=1, source_target_pairs={{1,0},{2,1},{3,2},{5,4},{6,5},{7,6}} | collective-permute-start | bytes 12582920 | tf_op jit(solution)/shard_map/while/body/eval_jaxpr/ppermute | solution.py:76
  3003.0 133.3 %collective-permute-start.1 = (bf16[1024,2048]{1,0:T(8,128)(2,1)}, bf16[1024,2048]{1,0:T(8,128)(2,1)}, u32[]{:S(2)}, u32[]{:S(2)}) collective-permute-start(bf16[1024,2048]{1,0:T(8,128)(2,1)} %get-tuple-element.698), channel_id=1, source_target_pairs={{1,0},{2,1},{3,2},{5,4},{6,5},{7,6}} | collective-permute-start | bytes 12582920 | tf_op jit(solution)/shard_map/while/body/eval_jaxpr/ppermute | solution.py:76
  3688.4 16.9 copy-start
Sparse Core Ops, SparseCore 0:
  3136.5 551.9 all-reduce.2
where the time goes:
time: 3740 us; the launch traced here: 3720 us
  matrix products  2580 us (69%)
  waiting for transfers between devices  775 us (21%)
  local copies, waits for them, and re-layouts  163 us (4%)
  other arithmetic  91.2 us (2%)
  starting transfers between devices  75 us (2%)
    psum x1, waiting for transfers between devices, body(): y = lax.psum(y, 'stage')  552 us
    dot_general x7, matrix products, _bwd_layer(): jnp.dot(u.astype(jnp.bfloat16).T, g, preferred_element_type=jnp.float32)  449 us
    dot_general x7, matrix products, _bwd_layer(): du = jnp.dot(g, w2.T, preferred_element_type=jnp.float32)  438 us
    dot_general x7, matrix products, _bwd_layer(): dw1 = jnp.dot(h.T, dz, preferred_element_type=jnp.float32)  427 us
    dot_general x7, matrix products, _fwd_layer(): z = jnp.dot(h, w1, preferred_element_type=jnp.float32)  337 us
    dot_general x7, matrix products, _fwd_layer(): jnp.dot(u, w2, preferred_element_type=jnp.float32)  325 us
    dot_general x7, matrix products, _bwd_layer(): jnp.dot(dz, w1.T, preferred_element_type=jnp.float32)  315 us
    dot_general x7, matrix products, _bwd_layer(): z = jnp.dot(h, w1, preferred_element_type=jnp.float32)  290 us
  transfers between devices with their start and end apart: 15, of which 7 were waited for; matrix products, arithmetic and copies ran while one was open for 26% of the time, Pallas kernels for 0%

commit v1 on v0

v1 whole, which is shorter than its diff:
```python
import functools

import jax
import jax.numpy as jnp
from jax import lax
from jax.experimental import pallas as pl
from jax.experimental.pallas import tpu as pltpu
from jax.sharding import PartitionSpec as P

MESH = pl.DeviceIdType.MESH
C0 = 0.7978845608028654
C1 = 0.044715
CH = 256
HT = 1024
LAG = 4
F32 = jnp.float32
BF16 = jnp.bfloat16


def _nn(a, b):
    return lax.dot_general(a, b, (((1,), (0,)), ((), ())), preferred_element_type=F32)


def _nt(a, b):
    return lax.dot_general(a, b, (((1,), (1,)), ((), ())), preferred_element_type=F32)


def _gelu_parts(z):
    z2 = z * z
    t = jnp.tanh(z * (C0 + (C0 * C1) * z2))
    p = 0.5 + 0.5 * t
    gp = p + (z * (0.5 - 0.5 * (t * t))) * (C0 + (3.0 * C0 * C1) * z2)
    return (z * p).astype(BF16), gp


def _pipe_kernel(nc, n_b, x, g, w1, w2, y, dx, hin, gin, u, dz, gp,
                 w1p, w2p, w1s, w2s, acc, inb, outb, gpe, gpo, ue, uo,
                 pin_sem, w1_sem, w2_sem, in_sem, save_sem, oue, ouo, oge, ogo, ige, igo,
                 snd, snd_b, loc, fwd, recv_h, recv_g, recv_y, recv_dx):
    s = lax.axis_index('stage')
    first, last = s == 0, s == 3
    n_ops = nc + n_b
    warm = 8 - 2 * s - s // 3
    pairs = nc - warm

    def peer(j):
        return {'stage': j}

    def op_of(k):
        r = k - warm
        half = r // 2
        odd = r - 2 * half
        early = k < warm
        late = r >= 2 * pairs
        is_f = early | ((odd == 1) & (r < 2 * pairs))
        c = jnp.where(early, k, jnp.where(late, k - nc, jnp.where(odd == 1, warm + half, half)))
        return is_f, c

    def w1_copy(t, slot):
        return pltpu.make_async_copy(w1.at[:, pl.ds(pl.multiple_of(t * HT, HT), HT)], w1s.at[slot], w1_sem.at[slot])

    def w2_copy(t, slot):
        return pltpu.make_async_copy(w2.at[pl.ds(pl.multiple_of(t * HT, HT), HT), :], w2s.at[slot], w2_sem.at[slot])

    def pin_w1(i):
        return pltpu.make_async_copy(w1.at[:, pl.ds((2 * i + 1) * HT, HT)], w1p.at[i], pin_sem.at[i])

    def pin_w2(i):
        return pltpu.make_async_copy(w2.at[pl.ds(2 * i * HT, HT), :], w2p.at[i], pin_sem.at[4 + i])

    def hid(ref, c, t):
        return ref.at[pl.ds(pl.multiple_of(c * CH, CH), CH), pl.ds(pl.multiple_of(t * HT, HT), HT)]

    def remote(src, dst, send, recv, j):
        return pltpu.make_async_remote_copy(src_ref=src, dst_ref=dst, send_sem=send, recv_sem=recv,
                                            device_id=peer(j), device_id_type=MESH)

    def wait_recv(dst, recv):
        remote(outb.at[0], dst, snd.at[0], recv, 0).wait_recv()

    def fetch_input(k):
        is_f, c = op_of(k)
        slot = lax.rem(k, 2)

        @pl.when(is_f & first)
        def _():
            pltpu.make_async_copy(x.at[c], inb.at[slot], in_sem.at[slot]).start()

        @pl.when(is_f & (s > 0))
        def _():
            wait_recv(hin.at[c], recv_h.at[c])
            pltpu.make_async_copy(hin.at[c], inb.at[slot], in_sem.at[slot]).start()

        @pl.when((~is_f) & last)
        def _():
            pltpu.make_async_copy(g.at[c], inb.at[slot], in_sem.at[slot]).start()

        @pl.when((~is_f) & (s < 3))
        def _():
            wait_recv(gin.at[c], recv_g.at[c])
            pltpu.make_async_copy(gin.at[c], inb.at[slot], in_sem.at[slot]).start()

        @pl.when(~is_f)
        def _():
            pltpu.make_async_copy(gp.at[c, 0], gpe.at[1], ige.at[1]).start()

    def free_out(k):
        slot = lax.rem(k, 2)

        @pl.when(k >= 2)
        def _():
            was_f, c = op_of(k - 2)
            edge = (was_f & last) | ((~was_f) & first)
            remote(outb.at[slot], hin.at[0], snd.at[slot], recv_h.at[0], 0).wait_send()

            @pl.when(edge)
            def _():
                remote(outb.at[slot], hin.at[0], snd_b.at[slot], recv_h.at[0], 0).wait_send()
                pltpu.make_async_copy(outb.at[slot], y.at[0], loc.at[slot]).wait()

    def out_u(ref, c, t, buf, slot, sem):
        return pltpu.make_async_copy(buf.at[slot], hid(ref, c, t), sem.at[slot])

    def out_gp(c, t, buf, slot, sem):
        return pltpu.make_async_copy(buf.at[slot], gp.at[c, t], sem.at[slot])

    def forward(k, c):
        slot = lax.rem(k, 2)
        pltpu.make_async_copy(x.at[0], inb.at[slot], in_sem.at[slot]).wait()

        @pl.when(first)
        def _():
            pltpu.make_async_copy(inb.at[slot], hin.at[c], save_sem.at[slot]).start()

        w1_copy(0, 0).wait()
        acc[...] = inb[slot].astype(F32)
        ub, gpv = _gelu_parts(_nn(inb[slot], w1s[0]))
        ue[1] = ub
        gpe[1] = gpv
        out_u(u, c, 0, ue, 1, oue).start()
        out_gp(c, 0, gpe, 1, oge).start()

        def body(b, _):
            p, q = lax.rem(b, 2), 1 - lax.rem(b, 2)

            @pl.when(k == 0)
            def _():
                for i in range(3):
                    @pl.when(b == i)
                    def _():
                        pin_w2(i).wait()
                        pin_w1(i).wait()

            w2_copy(2 * b + 1, p).wait()
            w1_copy(2 * b + 2, q).wait()

            @pl.when(b >= 1)
            def _():
                out_u(u, c, 2 * b - 2, ue, p, oue).wait()
                out_gp(c, 2 * b - 2, gpe, p, oge).wait()
                w2_copy(2 * b + 3, q).start()

            @pl.when(b == 2)
            def _():
                out_u(u, c, 1, uo, 0, ouo).wait()
                out_gp(c, 1, gpo, 0, ogo).wait()

            w1_copy(lax.rem(2 * b + 4, 8), p).start()
            acc[...] += _nn(ue[q], w2p[b])
            ub, gpv = _gelu_parts(_nn(inb[slot], w1p[b]))
            uo[p] = ub
            gpo[p] = gpv
            out_u(u, c, 2 * b + 1, uo, p, ouo).start()
            out_gp(c, 2 * b + 1, gpo, p, ogo).start()
            ub, gpv = _gelu_parts(_nn(inb[slot], w1s[q]))
            ue[p] = ub
            gpe[p] = gpv
            out_u(u, c, 2 * b + 2, ue, p, oue).start()
            out_gp(c, 2 * b + 2, gpe, p, oge).start()
            acc[...] += _nn(uo[p], w2s[p])
            return 0

        lax.fori_loop(0, 3, body, 0)

        @pl.when(k == 0)
        def _():
            pin_w2(3).wait()
            pin_w1(3).wait()

        w2_copy(7, 1).wait()
        out_u(u, c, 3, uo, 1, ouo).wait()
        out_gp(c, 3, gpo, 1, ogo).wait()
        out_u(u, c, 4, ue, 1, oue).wait()
        out_gp(c, 4, gpe, 1, oge).wait()
        free_out(k)

        @pl.when(first)
        def _():
            pltpu.make_async_copy(inb.at[slot], hin.at[c], save_sem.at[slot]).wait()

        @pl.when(k + 1 < n_ops)
        def _():
            fetch_input(k + 1)

        w1_copy(2, 1).start()
        w2_copy(1, 0).start()
        ub, gpv = _gelu_parts(_nn(inb[slot], w1p[3]))
        uo[1] = ub
        gpo[1] = gpv
        out_u(u, c, 7, uo, 1, ouo).start()
        out_gp(c, 7, gpo, 1, ogo).start()
        acc[...] += _nn(ue[0], w2p[3])
        outb[slot] = (acc[...] + _nn(uo[1], w2s[1])).astype(BF16)
        w2_copy(3, 1).start()

        @pl.when(s < 3)
        def _():
            remote(outb.at[slot], hin.at[c], snd.at[slot], recv_h.at[c], s + 1).start()

        @pl.when(last)
        def _():
            remote(outb.at[slot], y.at[c], snd.at[slot], recv_y.at[c], 1).start()
            remote(outb.at[slot], y.at[c], snd_b.at[slot], recv_y.at[c], 2).start()
            pltpu.make_async_copy(outb.at[slot], y.at[c], loc.at[slot]).start()

        out_u(u, c, 5, uo, 0, ouo).wait()
        out_gp(c, 5, gpo, 0, ogo).wait()
        out_u(u, c, 6, ue, 0, oue).wait()
        out_gp(c, 6, gpe, 0, oge).wait()
        out_u(u, c, 7, uo, 1, ouo).wait()
        out_gp(c, 7, gpo, 1, ogo).wait()

    def pass_on_y(c):
        return remote(y.at[c], y.at[c], fwd.at[c], recv_y.at[c], 0)

    def pass_on_dx(c):
        return remote(dx.at[c], dx.at[c], fwd.at[c], recv_dx.at[c], 3)

    def in_gp(c, t, buf, slot, sem):
        return pltpu.make_async_copy(gp.at[c, t], buf.at[slot], sem.at[slot])

    def backward(k, c):
        slot = lax.rem(k, 2)
        in_gp(c, 1, gpo, 0, igo).start()
        in_gp(c, 2, gpe, 0, ige).start()

        @pl.when(s == 1)
        def _():
            wait_recv(y.at[c], recv_y.at[c])
            pass_on_y(c).start()

        @pl.when((s == 2) & (c >= LAG))
        def _():
            wait_recv(dx.at[c - LAG], recv_dx.at[c - LAG])
            pass_on_dx(c - LAG).start()

        pltpu.make_async_copy(x.at[0], inb.at[slot], in_sem.at[slot]).wait()

        @pl.when(last)
        def _():
            pltpu.make_async_copy(inb.at[slot], gin.at[c], save_sem.at[slot]).start()

        in_gp(c, 0, gpe, 1, ige).wait()
        acc[...] = inb[slot].astype(F32)
        ue[1] = (_nt(inb[slot], w2p[0]) * gpe[1]).astype(BF16)
        out_u(dz, c, 0, ue, 1, oue).start()

        def body(b, _):
            p, q = lax.rem(b, 2), 1 - lax.rem(b, 2)
            w1_copy(2 * b, p).wait()
            w2_copy(2 * b + 1, p).wait()
            in_gp(c, 2 * b + 1, gpo, p, igo).wait()
            in_gp(c, 2 * b + 2, gpe, p, ige).wait()

            @pl.when(b >= 1)
            def _():
                out_u(dz, c, 2 * b - 2, ue, p, oue).wait()
                w1_copy(2 * b + 2, q).start()
                w2_copy(2 * b + 3, q).start()

            @pl.when(b == 2)
            def _():
                out_u(dz, c, 1, uo, 0, ouo).wait()

            in_gp(c, 2 * b + 3, gpo, q, igo).start()

            @pl.when(b < 2)
            def _():
                in_gp(c, 2 * b + 4, gpe, q, ige).start()

            acc[...] += _nt(ue[q], w1s[p])
            uo[p] = (_nt(inb[slot], w2s[p]) * gpo[p]).astype(BF16)
            out_u(dz, c, 2 * b + 1, uo, p, ouo).start()
            ue[p] = (_nt(inb[slot], w2p[b + 1]) * gpe[p]).astype(BF16)
            out_u(dz, c, 2 * b + 2, ue, p, oue).start()
            acc[...] += _nt(uo[p], w1p[b])
            return 0

        lax.fori_loop(0, 3, body, 0)
        w1_copy(6, 1).wait()
        w2_copy(7, 1).wait()
        in_gp(c, 7, gpo, 1, igo).wait()
        out_u(dz, c, 3, uo, 1, ouo).wait()
        out_u(dz, c, 4, ue, 1, oue).wait()
        free_out(k)

        @pl.when(last)
        def _():
            pltpu.make_async_copy(inb.at[slot], gin.at[c], save_sem.at[slot]).wait()

        @pl.when(k + 1 < n_ops)
        def _():
            fetch_input(k + 1)

        w1_copy(0, 0).start()
        w2_copy(1, 0).start()
        uo[1] = (_nt(inb[slot], w2s[1]) * gpo[1]).astype(BF16)
        out_u(dz, c, 7, uo, 1, ouo).start()
        acc[...] += _nt(ue[0], w1s[1])
        outb[slot] = (acc[...] + _nt(uo[1], w1p[3])).astype(BF16)
        w1_copy(2, 1).start()
        w2_copy(3, 1).start()

        @pl.when(s > 0)
        def _():
            remote(outb.at[slot], gin.at[c], snd.at[slot], recv_g.at[c], s - 1).start()

        @pl.when(first)
        def _():
            remote(outb.at[slot], dx.at[c], snd.at[slot], recv_dx.at[c], 2).start()
            remote(outb.at[slot], dx.at[c], snd_b.at[slot], recv_dx.at[c], 1).start()
            pltpu.make_async_copy(outb.at[slot], dx.at[c], loc.at[slot]).start()

        out_u(dz, c, 5, uo, 0, ouo).wait()
        out_u(dz, c, 6, ue, 0, oue).wait()
        out_u(dz, c, 7, uo, 1, ouo).wait()

    w1_copy(0, 0).start()
    for i in range(4):
        pin_w2(i).start()
        pin_w1(i).start()
        if i == 0:
            w2_copy(1, 0).start()
            w1_copy(2, 1).start()
        if i == 1:
            w2_copy(3, 1).start()
    barrier = pltpu.get_barrier_semaphore()
    for d in range(1, 4):
        pl.semaphore_signal(barrier, inc=1, device_id=peer(lax.rem(s + d, 4)), device_id_type=MESH)
    pl.semaphore_wait(barrier, 3)
    fetch_input(0)

    def step(k, _):
        is_f, c = op_of(k)

        @pl.when(is_f)
        def _():
            forward(k, c)

        @pl.when(~is_f)
        def _():
            backward(k, c)

        return 0

    lax.fori_loop(0, n_ops, step, 0)

    w1_copy(0, 0).wait()
    w1_copy(2, 1).wait()
    w2_copy(1, 0).wait()
    w2_copy(3, 1).wait()
    free_out(n_ops)
    free_out(n_ops + 1)

    def tail(c, _):
        @pl.when((s == 2) & (c >= n_b - LAG))
        def _():
            wait_recv(dx.at[c], recv_dx.at[c])
            pass_on_dx(c).start()

        @pl.when((s == 1) | (s == 3))
        def _():
            wait_recv(dx.at[c], recv_dx.at[c])

        @pl.when((s == 0) | (s == 2))
        def _():
            wait_recv(y.at[c], recv_y.at[c])

        return 0

    lax.fori_loop(0, nc, tail, 0)

    def drain(c, _):
        @pl.when(s == 1)
        def _():
            pass_on_y(c).wait_send()

        @pl.when(s == 2)
        def _():
            pass_on_dx(c).wait_send()

        return 0

    lax.fori_loop(0, nc, drain, 0)


def _pipe(x, g, w1, w2):
    tokens, d = x.shape
    h = w1.shape[1]
    nc, nt = tokens // CH, h // HT
    rows = jax.ShapeDtypeStruct((nc, CH, d), BF16)
    wide = jax.ShapeDtypeStruct((tokens, h), BF16)
    anyspec = pl.BlockSpec(memory_space=pl.ANY)
    dma = pltpu.SemaphoreType.DMA
    outs = pl.pallas_call(
        functools.partial(_pipe_kernel, nc, nc),
        out_shape=(rows, rows, rows, rows, wide, wide, jax.ShapeDtypeStruct((nc, nt, CH, HT), F32)),
        in_specs=[anyspec] * 4,
        out_specs=(anyspec,) * 7,
        scratch_shapes=[
            pltpu.VMEM((4, d, HT), BF16), pltpu.VMEM((4, HT, d), BF16),
            pltpu.VMEM((2, d, HT), BF16), pltpu.VMEM((2, HT, d), BF16),
            pltpu.VMEM((CH, d), F32), pltpu.VMEM((2, CH, d), BF16), pltpu.VMEM((2, CH, d), BF16),
            pltpu.VMEM((2, CH, HT), F32), pltpu.VMEM((2, CH, HT), F32),
            pltpu.VMEM((2, CH, HT), BF16), pltpu.VMEM((2, CH, HT), BF16),
            dma((8,)), dma((2,)), dma((2,)), dma((2,)), dma((2,)), dma((2,)), dma((2,)), dma((2,)), dma((2,)), dma((2,)), dma((2,)),
            dma((2,)), dma((2,)), dma((2,)), dma((nc,)), dma((nc,)), dma((nc,)), dma((nc,)), dma((nc,)),
        ],
        compiler_params=pltpu.CompilerParams(collective_id=0, has_side_effects=True, vmem_limit_bytes=67043328),
        cost_estimate=pl.CostEstimate(flops=8 * tokens * d * h, bytes_accessed=2 << 30, transcendentals=tokens * h),
        name='pipe',
    )(x.reshape(nc, CH, d), g.reshape(nc, CH, d), w1, w2)
    return outs


def solution(mesh):
    def body(x, g, w1, w2):
        n_mb, mb, d = x.shape
        y, dx, hin, gin, u, dz, _ = _pipe(x.reshape(n_mb * mb, d), g.reshape(n_mb * mb, d), w1[0], w2[0])
        hin, gin = hin.reshape(n_mb * mb, d), gin.reshape(n_mb * mb, d)
        dw2 = jnp.dot(u.T, gin, preferred_element_type=F32)
        dw1 = jnp.dot(hin.T, dz, preferred_element_type=F32)
        return y.reshape(x.shape), dx.reshape(x.shape), dw1[None], dw2[None]

    return jax.shard_map(body, mesh=mesh,
                         in_specs=(P('data'), P('data'), P('stage'), P('stage')),
                         out_specs=(P('data'), P('data'), P(('data', 'stage')), P(('data', 'stage'))),
                         check_vma=False)
```

time: 3740 us -> 1280 us (0.34)
  matrix products: 2580 us -> 307 us
  Pallas kernels: 0 us -> 940 us
  waiting for transfers between devices: 775 us -> 0 us
  local copies, waits for them, and re-layouts: 163 us -> 23 us
  other arithmetic: 91.2 us -> 0 us
  starting transfers between devices: 75 us -> 0 us
    dot_general x49 -> x2, matrix products: 2580 us -> 307 us  [the longest x1 153 us: body(): dw1 = jnp.dot(hin.T, dz, preferred_element_type=F32)]
    pallas_call x0 -> x1, Pallas kernels: none -> 940 us  [_pipe(): pl.pallas_call(functools.partial(_pipe_kernel, nc, nc), out_shape=(rows,...]
    psum x1 -> x0, waiting for transfers between devices: 552 us -> none  [body(): y = lax.psum(y, 'stage')]
    ppermute x14 -> x0, waiting for transfers between devices: 223 us -> none  [the longest x7 223 us: fwd_tick(): recv = lax.ppermute(h, 'stage', fwd_perm)]
    dynamic_slice x21 -> x0, local copies, waits for them, and re-layouts: 84.2 us -> none  [_put(): old = lax.dynamic_index_in_dim(buf, i, 0, keepdims=False)]
    ppermute x14 -> x0, starting transfers between devices: 75 us -> none  [the longest x7 66 us: bwd_tick(): recv = lax.ppermute(gh, 'stage', bwd_perm)]
    dynamic_update_slice x7 -> x0, other arithmetic: 58.9 us -> none  [_put(): return lax.dynamic_update_index_in_dim(buf, jnp.where(ok, val, old), i, 0)]
  transfers between devices with their start and end apart: 15 -> 0, of which waited for: 7 -> 0; matrix products, arithmetic and copies ran while one was open for 26% -> 0% of each run, Pallas kernels for 0% -> 0%
where the time goes in v1:
time: 1280 us; the launch traced here: 1270 us
  Pallas kernels  940 us (73%)
  matrix products  307 us (24%)
  local copies, waits for them, and re-layouts  23 us (2%)
    pallas_call x1, Pallas kernels, _pipe(): pl.pallas_call(functools.partial(_pipe_kernel, nc, nc), out_shape=(rows,...  940 us
    dot_general x1, matrix products, body(): dw1 = jnp.dot(hin.T, dz, preferred_element_type=F32)  153 us
    dot_general x1, matrix products, body(): dw2 = jnp.dot(u.T, gin, preferred_element_type=F32)  153 us

profile of v1, /device:TPU:7, one launch (start us, length us, event | category | flops | bytes accessed | tf_op | source)
XLA Modules:
  0.0 1270.8 jit_solution(12204574250458300571)
XLA Ops:
  0.6 940.2 %pipe.1 = (bf16[16,256,2048]{2,1,0:T(8,128)(2,1)}, bf16[16,256,2048]{2,1,0:T(8,128)(2,1)}, bf16[16,256,2048]{2,1,0:T(8,128)(2,1)}, bf16[16,256,2048]{2,1,0:T(8,1...) custom-call(bf16[16,256,2048]{2,1,0:T(8,128)(2,1)} %bitcast.20, ...), custom_call_target="tpu_custom_call" | custom-call | flops 549755813888 | bytes 2147483648 | tf_op jit(solution)/shard_map/pipe/pallas_call | solution.py:415
  940.8 153.3 %convolution_bitcast_fusion = f32[1,2048,8192]{2,1,0:T(8,128)} fusion(bf16[4096,2048]{1,0:T(8,128)(2,1)} %bitcast.23, bf16[4096,8192]{1,0:T(8,128)(2,1)} %get-tuple-element.13), kind=kOutput, calls=%fused_computation | convolution fusion | flops 137438953472 | bytes 150994944 | tf_op jit(solution)/shard_map/dot_general | solution.py:442
  1094.1 153.2 %convolution_bitcast_fusion.1 = f32[1,8192,2048]{2,1,0:T(8,128)} fusion(bf16[4096,8192]{1,0:T(8,128)(2,1)} %get-tuple-element.14, bf16[4096,2048]{1,0:T(8,128)(2,1)} %bitcast.22), kind=kOutput, calls=%fused_computation.1 | convolution fusion | flops 137438953472 | bytes 150994944 | tf_op jit(solution)/shard_map/dot_general | solution.py:441
  1247.4 0.0 copy-start
  1247.4 15.1 %copy.10 = bf16[4,1024,2048]{2,1,0:T(8,128)(2,1)} copy(bf16[4,1024,2048]{2,1,0:T(8,128)(2,1)} %bitcast.17) | data formatting | bytes 33554432
  1262.4 1.8 copy-done
  1264.2 6.2 copy.11
Async XLA Ops:
  1247.4 16.9 %copy-start = (bf16[16,256,2048]{2,1,0:T(8,128)(2,1)S(1)}, bf16[16,256,2048]{2,1,0:T(8,128)(2,1)}, u32[]{:S(2)}) copy-start(bf16[16,256,2048]{2,1,0:T(8,128)(2,1)} %get-tuple-element.11) | copy-start | bytes 50331652

commit v2 on v1

v2 whole, which is shorter than its diff:
```python
import functools

import jax
import jax.numpy as jnp
from jax import lax
from jax.experimental import pallas as pl
from jax.experimental.pallas import tpu as pltpu
from jax.sharding import PartitionSpec as P

MESH = pl.DeviceIdType.MESH
C0 = 0.7978845608028654
C1 = 0.044715
CH = 256
HT = 1024
DX_OP = 18
Y_FIRST = 12
Y_BLOCK = 3
EARLY = (8, 6, 2, 0)
VMEM_MAX = 67043328
F32 = jnp.float32
BF16 = jnp.bfloat16


def _nn(a, b):
    return lax.dot_general(a, b, (((1,), (0,)), ((), ())), preferred_element_type=F32)


def _nt(a, b):
    return lax.dot_general(a, b, (((1,), (1,)), ((), ())), preferred_element_type=F32)


def _tn(a, b):
    return lax.dot_general(a, b, (((0,), (0,)), ((), ())), preferred_element_type=F32)


def _gelu_parts(z):
    z2 = z * z
    p = jax.nn.sigmoid(z * (2.0 * C0 + (2.0 * C0 * C1) * z2))
    gu = z * p
    gp = p + (gu * (1.0 - p)) * (2.0 * C0 + (6.0 * C0 * C1) * z2)
    return gu.astype(BF16), gp


def _pipe_kernel(n_f, b0, n_b, *refs):
    if n_f:
        x, g, w1, w2, y, dx, hin, gin, u, dz, gp = refs[:11]
        part = None
        scratch = refs[11:]
    else:
        g, w1, w2, gp, u, _, _, _, _, _, y, dx, gin, dz, part = refs[:15]
        x = hin = None
        scratch = refs[15:]
    fwd, recv_y, recv_dx, more = scratch[15:19]
    _chunks(n_f, b0, n_b, x, g, w1, w2, y, dx, hin, gin, u, dz, gp, part, *scratch)
    s = lax.axis_index('stage')
    row, remote, wait_recv = _moves()
    n_ops = n_f + n_b
    dx_from = (n_ops - DX_OP + 1) // 2 if n_f else 0
    y0, n_y = (0, Y_FIRST) if n_f else (Y_FIRST, (b0 + n_b) - Y_FIRST)
    y_from = n_b if n_f else 0

    def tail_y(j, _):
        c = y0 + j

        @pl.when((s == 1) & (j >= y_from))
        def _():
            wait_recv(row(y, c), recv_y.at[j])
            remote(row(y, c), row(y, c), fwd.at[j], recv_y.at[j], 0).start()

        @pl.when((s == 0) | (s == 2))
        def _():
            wait_recv(row(y, c), recv_y.at[j])

        return 0

    def tail_dx(j, _):
        c = b0 + j

        @pl.when((s == 2) & (j >= dx_from))
        def _():
            wait_recv(row(dx, c), recv_dx.at[j])
            remote(row(dx, c), row(dx, c), fwd.at[j], recv_dx.at[j], 3).start()

        @pl.when((s == 1) | (s == 3))
        def _():
            wait_recv(row(dx, c), recv_dx.at[j])

        return 0

    lax.fori_loop(0, n_y, tail_y, 0)
    lax.fori_loop(0, n_b, tail_dx, 0)

    def drain(j, _):
        @pl.when(((s == 1) & (j < n_y)) | ((s == 2) & (j < n_b)))
        def _():
            remote(row(y, 0), row(y, 0), fwd.at[j], recv_y.at[j], 0).wait_send()

        if not n_f:
            @pl.when((s == 3) & (j < n_y))
            def _():
                remote(row(y, 0), row(y, 0), fwd.at[j], recv_y.at[j], 0).wait_send()
                remote(row(y, 0), row(y, 0), more.at[j], recv_y.at[j], 0).wait_send()

        return 0

    lax.fori_loop(0, max(n_y, n_b), drain, 0)


def _moves():
    def row(ref, c):
        return ref.at[pl.ds(pl.multiple_of(c * CH, CH), CH), :]

    def remote(src, dst, send, recv, j):
        return pltpu.make_async_remote_copy(src_ref=src, dst_ref=dst, send_sem=send, recv_sem=recv,
                                            device_id={'stage': j}, device_id_type=MESH)

    def wait_recv(dst, recv):
        remote(dst, dst, recv, recv, 0).wait_recv()

    return row, remote, wait_recv


def _per_stage(s, counts):
    return sum(jnp.where(s == i, c, 0) for i, c in enumerate(counts))


def _chunks(n_f, b0, n_b, x, g, w1, w2, y, dx, hin, gin, u, dz, gp, part,
            pin_sem, w1_sem, w2_sem, in_sem, save_sem, oue, ouo, oge, ogo, ige, igo,
            snd, snd_b, loc, recv_g, fwd, recv_y, recv_dx, more,
            w1p, w2p, w1s, w2s, acc, inb, outb, gpe, gpo, ue, uo):
    recv_h = more
    row, remote, wait_recv = _moves()
    s = lax.axis_index('stage')
    first, last = s == 0, s == 3
    n_ops = n_f + n_b
    if n_f:
        warm = 16 - 4 * s - 4 * (s // 2) + (s // 3)
        pairs = jnp.minimum(n_b, n_f - warm)

    def peer(j):
        return {'stage': j}

    def op_of(k):
        if not n_f:
            return False, b0 + k
        r = k - warm
        half = r // 2
        odd = r - 2 * half
        early = k < warm
        late = r >= 2 * pairs
        late_f = warm + pairs < n_f
        is_f = early | ((odd == 1) & (~late)) | (late & late_f)
        c_late = jnp.where(late_f, warm + pairs, pairs) + r - 2 * pairs
        c = jnp.where(early, k, jnp.where(late, c_late, jnp.where(odd == 1, warm + half, half)))
        return is_f, c

    def w1_copy(t, slot):
        return pltpu.make_async_copy(w1.at[:, pl.ds(pl.multiple_of(t * HT, HT), HT)], w1s.at[slot], w1_sem.at[slot])

    def w2_copy(t, slot):
        return pltpu.make_async_copy(w2.at[pl.ds(pl.multiple_of(t * HT, HT), HT), :], w2s.at[slot], w2_sem.at[slot])

    def pin_w1(i):
        return pltpu.make_async_copy(w1.at[:, pl.ds((2 * i + 1) * HT, HT)], w1p.at[i], pin_sem.at[i])

    def pin_w2(i):
        return pltpu.make_async_copy(w2.at[pl.ds(2 * i * HT, HT), :], w2p.at[i], pin_sem.at[4 + i])

    def wait_pins(k, b):
        @pl.when(k == 0)
        def _():
            for i in range(3):
                @pl.when(b == i)
                def _():
                    pin_w2(i if n_f else i + 1).wait()
                    pin_w1(i).wait()

    def hid(ref, c, t):
        return ref.at[pl.ds(pl.multiple_of(c * CH, CH), CH), pl.ds(pl.multiple_of(t * HT, HT), HT)]

    def load_input(ref, c, slot):
        return pltpu.make_async_copy(row(ref, c), inb.at[slot], in_sem.at[slot])

    def fetch_input(k):
        is_f, c = op_of(k)
        slot = lax.rem(k, 2)
        is_b = True if not n_f else ~is_f
        if n_f:
            @pl.when(is_f & first)
            def _():
                load_input(x, c, slot).start()

            @pl.when(is_f & (s > 0))
            def _():
                wait_recv(row(hin, c), recv_h.at[c])
                load_input(hin, c, slot).start()

        @pl.when(is_b & last)
        def _():
            load_input(g, c, slot).start()

        @pl.when(is_b & (s < 3))
        def _():
            wait_recv(row(gin, c), recv_g.at[c])
            load_input(gin, c, slot).start()

        @pl.when(is_b)
        def _():
            in_gp(c, 0, *place(0)).start()

    def exits(k):
        is_f, c = op_of(k)
        if not n_f:
            return True, first, first
        share = (is_f & last & (c < Y_FIRST)) | ((~is_f) & first)
        own = (is_f & last) | ((~is_f) & first)
        return share | (~own), share, own

    def free_out(k):
        slot = lax.rem(k, 2)

        @pl.when(k >= 2)
        def _():
            one, two, own = exits(k - 2)

            @pl.when(one)
            def _():
                remote(outb.at[slot], row(gin, 0), snd.at[slot], recv_g.at[0], 0).wait_send()

            @pl.when(two)
            def _():
                remote(outb.at[slot], row(gin, 0), snd_b.at[slot], recv_g.at[0], 0).wait_send()

            @pl.when(own)
            def _():
                pltpu.make_async_copy(outb.at[slot], row(dx, 0), loc.at[slot]).wait()

    def place(t):
        return t % 2, (t - 1) // 2 % 2

    def out_u(ref, c, t, odd, slot):
        return pltpu.make_async_copy((ue, uo)[odd].at[slot], hid(ref, c, t), (oue, ouo)[odd].at[slot])

    def out_gp(c, t, odd, slot):
        return pltpu.make_async_copy((gpe, gpo)[odd].at[slot], gp.at[c, t], (oge, ogo)[odd].at[slot])

    def in_gp(c, t, odd, slot):
        return pltpu.make_async_copy(gp.at[c, t], (gpe, gpo)[odd].at[slot], (ige, igo)[odd].at[slot])

    def flush(ref, c, *tiles):
        for t in tiles:
            out_u(ref, c, t, *place(t)).wait()
            if ref is not dz:
                out_gp(c, t, *place(t)).wait()

    def emit(c, t, odd, slot):
        out_u(u, c, t, odd, slot).start()
        out_gp(c, t, odd, slot).start()

    def forward(k, c):
        slot = lax.rem(k, 2)
        load_input(x, 0, slot).wait()

        @pl.when(first)
        def _():
            pltpu.make_async_copy(inb.at[slot], row(hin, c), save_sem.at[slot]).start()

        w1_copy(0, 0).wait()
        acc[...] = inb[slot].astype(F32)
        ub, gpv = _gelu_parts(_nn(inb[slot], w1s[0]))
        ue[1] = ub
        gpe[1] = gpv
        emit(c, 0, *place(0))

        def body(b, _):
            p, q = lax.rem(b, 2), 1 - lax.rem(b, 2)
            wait_pins(k, b)
            w2_copy(2 * b + 1, p).wait()
            w1_copy(2 * b + 2, q).wait()

            @pl.when(b >= 1)
            def _():
                out_u(u, c, 2 * b - 2, 0, p).wait()
                out_gp(c, 2 * b - 2, 0, p).wait()
                w2_copy(2 * b + 3, q).start()

            @pl.when(b == 2)
            def _():
                flush(u, c, 1)

            w1_copy(lax.rem(2 * b + 4, 8), p).start()
            acc[...] += _nn(ue[q], w2p[b])
            ub, gpv = _gelu_parts(_nn(inb[slot], w1p[b]))
            uo[p] = ub
            gpo[p] = gpv
            ub, gpv = _gelu_parts(_nn(inb[slot], w1s[q]))
            ue[p] = ub
            gpe[p] = gpv
            acc[...] += _nn(uo[p], w2s[p])
            emit(c, 2 * b + 1, 1, p)
            emit(c, 2 * b + 2, 0, p)
            return 0

        lax.fori_loop(0, 3, body, 0)

        @pl.when(k == 0)
        def _():
            pin_w2(3).wait()
            pin_w1(3).wait()

        w2_copy(7, 1).wait()
        flush(u, c, 3, 4)
        free_out(k)

        @pl.when(first)
        def _():
            pltpu.make_async_copy(inb.at[slot], row(hin, c), save_sem.at[slot]).wait()

        @pl.when((k > 0) & (k + 1 < n_ops) & (k + 1 != warm))
        def _():
            fetch_input(k + 1)

        w2_copy(1, 0).start()
        w1_copy(2, 1).start()
        ub, gpv = _gelu_parts(_nn(inb[slot], w1p[3]))
        uo[1] = ub
        gpo[1] = gpv
        emit(c, 7, *place(7))
        acc[...] += _nn(ue[0], w2p[3])
        outb[slot] = (acc[...] + _nn(uo[1], w2s[1])).astype(BF16)

        @pl.when(s < 3)
        def _():
            remote(outb.at[slot], row(hin, c), snd.at[slot], recv_h.at[c], s + 1).start()

        @pl.when(last)
        def _():
            pltpu.make_async_copy(outb.at[slot], row(y, c), loc.at[slot]).start()

            @pl.when(c < Y_FIRST)
            def _():
                remote(outb.at[slot], row(y, c), snd.at[slot], recv_y.at[c], 1).start()
                remote(outb.at[slot], row(y, c), snd_b.at[slot], recv_y.at[c], 2).start()

        flush(u, c, 5, 6, 7)

        @pl.when((k == 0) | (k + 1 == warm))
        def _():
            fetch_input(k + 1)

        first_gp(k + 1)
        w2_copy(3, 1).start()

    def first_gp(k):
        is_f, c = op_of(k)

        @pl.when((k < n_ops) & (True if not n_f else ~is_f))
        def _():
            for t in (1, 2):
                in_gp(c, t, *place(t)).start()

    def pass_on_y(c):
        wait_recv(row(y, c), recv_y.at[c])
        remote(row(y, c), row(y, c), fwd.at[c], recv_y.at[c], 0).start()

    def backward(k, c):
        slot = lax.rem(k, 2)
        if n_f:
            @pl.when(s == 1)
            def _():
                pass_on_y(c)
        load_input(g, 0, slot).wait()

        @pl.when(last)
        def _():
            pltpu.make_async_copy(inb.at[slot], row(gin, c), save_sem.at[slot]).start()

        in_gp(c, 0, *place(0)).wait()
        if not n_f:
            @pl.when(k == 0)
            def _():
                pin_w2(0).wait()
        acc[...] = inb[slot].astype(F32)
        ue[1] = (_nt(inb[slot], w2p[0]) * gpe[1]).astype(BF16)
        out_u(dz, c, 0, *place(0)).start()

        def body(b, _):
            p, q = lax.rem(b, 2), 1 - lax.rem(b, 2)
            if not n_f:
                wait_pins(k, b)
            w1_copy(2 * b, p).wait()
            w2_copy(2 * b + 1, p).wait()
            in_gp(c, 2 * b + 1, 1, p).wait()
            in_gp(c, 2 * b + 2, 0, p).wait()

            @pl.when(b >= 1)
            def _():
                out_u(dz, c, 2 * b - 2, 0, p).wait()

            @pl.when(b == 2)
            def _():
                flush(dz, c, 1)

            in_gp(c, 2 * b + 3, 1, q).start()

            @pl.when(b < 2)
            def _():
                in_gp(c, 2 * b + 4, 0, q).start()

            @pl.when(b >= 1)
            def _():
                w1_copy(2 * b + 2, q).start()
                w2_copy(2 * b + 3, q).start()

            acc[...] += _nt(ue[q], w1s[p])
            uo[p] = (_nt(inb[slot], w2s[p]) * gpo[p]).astype(BF16)
            out_u(dz, c, 2 * b + 1, 1, p).start()
            ue[p] = (_nt(inb[slot], w2p[b + 1]) * gpe[p]).astype(BF16)
            out_u(dz, c, 2 * b + 2, 0, p).start()
            acc[...] += _nt(uo[p], w1p[b])
            return 0

        lax.fori_loop(0, 3, body, 0)
        if not n_f:
            @pl.when(k == 0)
            def _():
                pin_w1(3).wait()
        w1_copy(6, 1).wait()
        w2_copy(7, 1).wait()
        in_gp(c, 7, *place(7)).wait()
        flush(dz, c, 3, 4)
        free_out(k)

        @pl.when(last)
        def _():
            pltpu.make_async_copy(inb.at[slot], row(gin, c), save_sem.at[slot]).wait()

        @pl.when(k + 1 < n_ops)
        def _():
            fetch_input(k + 1)

        w1_copy(0, 0).start()
        w2_copy(1, 0).start()
        uo[1] = (_nt(inb[slot], w2s[1]) * gpo[1]).astype(BF16)
        out_u(dz, c, 7, *place(7)).start()
        acc[...] += _nt(ue[0], w1s[1])
        outb[slot] = (acc[...] + _nt(uo[1], w1p[3])).astype(BF16)
        if not n_f:
            @pl.when(k == 0)
            def _():
                pl.semaphore_wait(barrier, 2 - (s == 1).astype(jnp.int32))

        @pl.when(s > 0)
        def _():
            remote(outb.at[slot], row(gin, c), snd.at[slot], recv_g.at[c], s - 1).start()

        @pl.when(first)
        def _():
            pltpu.make_async_copy(outb.at[slot], row(dx, c), loc.at[slot]).start()
            remote(outb.at[slot], row(dx, c), snd.at[slot], recv_dx.at[c - b0], 2).start()
            remote(outb.at[slot], row(dx, c), snd_b.at[slot], recv_dx.at[c - b0], 1).start()

        first_gp(k + 1)
        w1_copy(2, 1).start()
        w2_copy(3, 1).start()
        flush(dz, c, 5, 6, 7)

    def half_blocks(lo, hi):
        half = w1p.shape[1]

        def g_copy(i):
            return pltpu.make_async_copy(gin.at[pl.ds(0, half), pl.ds(i * HT, HT)], w1p.at[i], pin_sem.at[i])

        def u_copy(i, slot):
            return pltpu.make_async_copy(u.at[pl.ds(0, half), pl.ds(pl.multiple_of(i * HT, HT), HT)], w1s.at[slot], w1_sem.at[slot])

        def out(i, j, p, buf, col, sem):
            rows = pl.ds(pl.multiple_of(i * HT + j * CH, CH), CH)
            return pltpu.make_async_copy(buf.at[p], part.at[rows, pl.ds(col * HT, HT)], sem.at[p])

        @pl.when(lo < hi)
        def _():
            u_copy(lo, 0).start()
            g_copy(0).start()
            g_copy(1).start()
            g_copy(0).wait()
            g_copy(1).wait()

            def block(i, _):
                slot = lax.rem(i - lo, 2)

                @pl.when(i + 1 < hi)
                def _():
                    u_copy(i + 1, 1 - slot).start()

                u_copy(i, slot).wait()

                @pl.when(last & (i == lo + Y_BLOCK))
                def _():
                    for j in range(b0 + n_b - Y_FIRST):
                        yj = row(y, Y_FIRST + j)
                        remote(yj, yj, fwd.at[j], recv_y.at[j], 1).start()
                        remote(yj, yj, more.at[j], recv_y.at[j], 2).start()

                def strips(jj, _):
                    @pl.when((i > lo) | (jj > 0))
                    def _():
                        for p in range(2):
                            out(i, 0, p, gpe, 0, oge).wait()
                            out(i, 0, p, gpo, 1, ogo).wait()

                    for p in range(2):
                        inb[p] = w1s[slot, :, pl.ds(pl.multiple_of((2 * jj + p) * CH, CH), CH)].T
                    for p in range(2):
                        gpe[p] = _nn(inb[p], w1p[0])
                        gpo[p] = _nn(inb[p], w1p[1])
                        out(i, 2 * jj + p, p, gpe, 0, oge).start()
                        out(i, 2 * jj + p, p, gpo, 1, ogo).start()
                    return 0

                lax.fori_loop(0, HT // CH // 2, strips, 0)
                return 0

            lax.fori_loop(lo, hi, block, 0)
            for p in range(2):
                out(lo, 0, p, gpe, 0, oge).wait()
                out(lo, 0, p, gpo, 1, ogo).wait()

    barrier = pltpu.get_barrier_semaphore()
    if n_f:
        @pl.when(first)
        def _():
            fetch_input(0)
        w1_copy(0, 0).start()
        for i in range(4):
            pin_w2(i).start()
            pin_w1(i).start()
            if i == 0:
                w2_copy(1, 0).start()
                w1_copy(2, 1).start()
            if i == 1:
                w2_copy(3, 1).start()
        for d in range(1, 4):
            pl.semaphore_signal(barrier, inc=1, device_id=peer(lax.rem(s + d, 4)), device_id_type=MESH)
        pl.semaphore_wait(barrier, 3)

        @pl.when(s > 0)
        def _():
            fetch_input(0)
    else:
        for to, frm in ((1, 0), (2, 1), (3, 1), (0, 1), (3, 2), (0, 2), (2, 3)):
            @pl.when(s == frm)
            def _():
                pl.semaphore_signal(barrier, inc=1, device_id=peer(to), device_id_type=MESH)
        @pl.when(last)
        def _():
            fetch_input(0)
        pin_w2(0).start()
        w1_copy(0, 0).start()
        w2_copy(1, 0).start()
        pin_w1(0).start()
        pin_w2(1).start()
        first_gp(0)
        w1_copy(2, 1).start()
        w2_copy(3, 1).start()
        for i in range(1, 4):
            pin_w1(i).start()
            if i < 3:
                pin_w2(i + 1).start()

        @pl.when(s < 3)
        def _():
            fetch_input(0)

    def step(k, _):
        is_f, c = op_of(k)
        if not n_f:
            backward(k, c)
            return 0
        gone = k - DX_OP
        cd = gone // 2

        @pl.when((s == 2) & (gone >= 0) & (gone == 2 * cd) & (gone < 2 * n_b))
        def _():
            wait_recv(row(dx, cd), recv_dx.at[cd])
            remote(row(dx, cd), row(dx, cd), fwd.at[cd], recv_dx.at[cd], 3).start()

        @pl.when(is_f)
        def _():
            forward(k, c)

        @pl.when(~is_f)
        def _():
            backward(k, c)

        return 0

    lax.fori_loop(0, n_ops, step, 0)

    w1_copy(0, 0).wait()
    w1_copy(2, 1).wait()
    w2_copy(1, 0).wait()
    w2_copy(3, 1).wait()
    free_out(n_ops)
    free_out(n_ops + 1)
    if not n_f:
        half_blocks(_per_stage(s, EARLY), u.shape[1] // HT)


def _scratch(nc, n_b, d, n_f):
    dma = pltpu.SemaphoreType.DMA
    sems = [dma((8,)), *[dma((2,))] * 13, *[dma((nc,))] * 5]
    return sems + [
        pltpu.VMEM((4, d, HT), BF16), pltpu.VMEM((4, HT, d), BF16),
        pltpu.VMEM((2, d, HT), BF16), pltpu.VMEM((2, HT, d), BF16),
        pltpu.VMEM((CH, d), F32), pltpu.VMEM((2, CH, d), BF16), pltpu.VMEM((2, CH, d), BF16),
        pltpu.VMEM((2, CH, HT), F32), pltpu.VMEM((2, CH, HT), F32),
        pltpu.VMEM((2, CH, HT), BF16), pltpu.VMEM((2, CH, HT), BF16)]


def _first_kernel(x, g, w1, w2, n_b):
    tokens, d = x.shape
    h = w1.shape[1]
    nc = tokens // CH
    rows = jax.ShapeDtypeStruct((tokens, d), BF16)
    wide = jax.ShapeDtypeStruct((tokens, h), BF16)
    anyspec = pl.BlockSpec(memory_space=pl.ANY)
    return pl.pallas_call(
        functools.partial(_pipe_kernel, nc, 0, n_b),
        out_shape=(rows, rows, rows, rows, wide, wide, jax.ShapeDtypeStruct((nc, h // HT, CH, HT), F32)),
        in_specs=[anyspec] * 4,
        out_specs=(anyspec,) * 7,
        scratch_shapes=_scratch(nc, n_b, d, nc),
        compiler_params=pltpu.CompilerParams(collective_id=0, has_side_effects=True, vmem_limit_bytes=VMEM_MAX),
        cost_estimate=pl.CostEstimate(flops=4 * (nc + n_b) * CH * d * h, bytes_accessed=1 << 30, transcendentals=0),
        name='pipe_a',
    )(x, g, w1, w2)


def _second_kernel(g, w1, w2, gp, u, y, dx, gin, dz, part, b0):
    tokens, d = g.shape
    h = w1.shape[1]
    nc = tokens // CH
    n_b = nc - b0
    anyspec = pl.BlockSpec(memory_space=pl.ANY)
    return pl.pallas_call(
        functools.partial(_pipe_kernel, 0, b0, n_b),
        out_shape=tuple(jax.ShapeDtypeStruct(a.shape, a.dtype) for a in (y, dx, gin, dz, part)),
        in_specs=[anyspec] * 10,
        out_specs=(anyspec,) * 5,
        scratch_shapes=_scratch(nc, n_b, d, 0),
        input_output_aliases={5 + i: i for i in range(5)},
        compiler_params=pltpu.CompilerParams(collective_id=1, has_side_effects=True, vmem_limit_bytes=VMEM_MAX),
        cost_estimate=pl.CostEstimate(flops=4 * n_b * CH * d * h, bytes_accessed=1 << 29, transcendentals=0),
        name='pipe_b',
    )(g, w1, w2, gp, u, y, dx, gin, dz, part)


def _half_blocks(lo, n, half, u, g, o):
    def block(u_ref, g_ref, o_ref):
        o_ref[...] = _tn(u_ref[...], g_ref[...])

    d = g.shape[1]
    pltpu.emit_pipeline(
        block, grid=(n,),
        in_specs=[pl.BlockSpec((half, 1024), lambda i: (0, lo + i)), pl.BlockSpec((half, d), lambda i: (0, 0))],
        out_specs=[pl.BlockSpec((1024, d), lambda i: (lo + i, 0))])(u, g, o)


def _early_kernel(half, u, g, o):
    n = _per_stage(lax.axis_index('stage'), EARLY)

    @pl.when(n > 0)
    def _():
        _half_blocks(0, n, half, u, g, o)


def _early_dw2(u, gin, half):
    tokens, h = u.shape
    d = gin.shape[1]
    anyspec = pl.BlockSpec(memory_space=pl.ANY)
    return pl.pallas_call(
        functools.partial(_early_kernel, half),
        in_specs=[anyspec] * 2,
        out_specs=anyspec,
        out_shape=jax.ShapeDtypeStruct((h, d), F32),
        compiler_params=pltpu.CompilerParams(vmem_limit_bytes=VMEM_MAX),
        cost_estimate=pl.CostEstimate(flops=half * d * h, bytes_accessed=1 << 26, transcendentals=0),
        name='early_dw2',
    )(u, gin)


def _dw2_kernel(u_ref, g_ref, part_ref, y_ref, o_ref, yo_ref):
    yo_ref[...] = y_ref[...]
    o_ref[...] = part_ref[...] + _tn(u_ref[...], g_ref[...])


def _dw2(u, gin, part, y, half):
    tokens, h = u.shape
    d = gin.shape[1]
    steps = h // 1024
    rows = pl.BlockSpec((tokens // steps, d), lambda i: (i, 0))
    blocks = pl.BlockSpec((1024, d), lambda i: (i, 0))
    return pl.pallas_call(
        _dw2_kernel,
        grid=(steps,),
        in_specs=[pl.BlockSpec((half, 1024), lambda i: (1, i)),
                  pl.BlockSpec((half, d), lambda i: (1, 0), pipeline_mode=pl.Buffered(1)), blocks, rows],
        out_specs=(blocks, rows),
        out_shape=(jax.ShapeDtypeStruct((h, d), F32), jax.ShapeDtypeStruct(y.shape, BF16)),
        compiler_params=pltpu.CompilerParams(vmem_limit_bytes=VMEM_MAX, dimension_semantics=('arbitrary',)),
        cost_estimate=pl.CostEstimate(flops=tokens * d * h, bytes_accessed=1 << 27, transcendentals=0),
        name='dw2',
    )(u, gin, part, y)


def _dw1_kernel(h_ref, z_ref, x_ref, o_ref, xo_ref):
    xo_ref[...] = x_ref[...]
    o_ref[...] = _tn(h_ref[...], z_ref[...])


def _dw1(hin, dz, dx):
    tokens, d = hin.shape
    h = dz.shape[1]
    nj = h // 1024
    rows = pl.BlockSpec((tokens // (nj * (d // 1024)), d), lambda i, j: (i * nj + j, 0))
    return pl.pallas_call(
        _dw1_kernel,
        grid=(d // 1024, nj),
        in_specs=[pl.BlockSpec((tokens, 1024), lambda i, j: (0, i)), pl.BlockSpec((tokens, 1024), lambda i, j: (0, j)), rows],
        out_specs=(pl.BlockSpec((1024, 1024), lambda i, j: (i, j)), rows),
        out_shape=(jax.ShapeDtypeStruct((d, h), F32), jax.ShapeDtypeStruct(dx.shape, BF16)),
        compiler_params=pltpu.CompilerParams(vmem_limit_bytes=VMEM_MAX, dimension_semantics=('arbitrary', 'arbitrary')),
        cost_estimate=pl.CostEstimate(flops=2 * tokens * d * h, bytes_accessed=1 << 27, transcendentals=0),
        name='dw1',
    )(hin, dz, dx)


def solution(mesh):
    def body(x, g, w1, w2):
        n_mb, mb, d = x.shape
        tokens = n_mb * mb
        b0 = tokens // CH // 2
        xt, gt = x.reshape(tokens, d), g.reshape(tokens, d)
        y, dx, hin, gin, u, dz, gp = _first_kernel(xt, gt, w1[0], w2[0], b0)
        part = _early_dw2(u, gin, tokens // 2)
        y, dx, gin, dz, part = _second_kernel(gt, w1[0], w2[0], gp, u, y, dx, gin, dz, part, b0)
        dw2, y = _dw2(u, gin, part, y, tokens // 2)
        dw1, dx = _dw1(hin, dz, dx)
        return y.reshape(x.shape), dx.reshape(x.shape), dw1[None], dw2[None]

    return jax.shard_map(body, mesh=mesh,
                         in_specs=(P('data'), P('data'), P('stage'), P('stage')),
                         out_specs=(P('data'), P('data'), P(('data', 'stage')), P(('data', 'stage'))),
                         check_vma=False)
```

time: 1280 us -> 1160 us (0.906)
  matrix products: 307 us -> 0 us
  Pallas kernels: 940 us -> 1150 us
  local copies, waits for them, and re-layouts: 23 us -> 0 us
    dot_general x2 -> x0, matrix products: 307 us -> none  [the longest x1 153 us: body(): dw1 = jnp.dot(hin.T, dz, preferred_element_type=F32)]
    pallas_call x1 -> x5, Pallas kernels: 940 us -> 1150 us  [the longest x1 629 us: _first_kernel(): pl.pallas_call(functools.partial(_pipe_kernel, nc, 0, n_b), out_shape=(ro...]
    unnamed x4 -> x0, local copies, waits for them, and re-layouts: 23 us -> none
where the time goes in v2:
time: 1160 us
  Pallas kernels  1150 us (99%)
    pallas_call x1, Pallas kernels, _first_kernel(): pl.pallas_call(functools.partial(_pipe_kernel, nc, 0, n_b), out_shape=(ro...  629 us
    pallas_call x1, Pallas kernels, _second_kernel(): pl.pallas_call(functools.partial(_pipe_kernel, 0, b0, n_b), out_shape=tup...  289 us
    pallas_call x1, Pallas kernels, _dw1(): pl.pallas_call(_dw1_kernel, grid=(d // 1024, nj), in_specs=[pl.BlockSpec(...  151 us
    pallas_call x1, Pallas kernels, _dw2(): pl.pallas_call(_dw2_kernel, grid=(steps,), in_specs=[pl.BlockSpec((half,...  85.8 us

profile of v2, /device:TPU:7, one launch (start us, length us, event | category | flops | bytes accessed | tf_op | source)
XLA Modules:
  0.0 1155.6 jit_solution(9631089117785328559)
XLA Ops:
  0.6 628.6 %pipe_a.1 = (bf16[4096,2048]{1,0:T(8,128)(2,1)}, bf16[4096,2048]{1,0:T(8,128)(2,1)}, bf16[4096,2048]{1,0:T(8,128)(2,1)}, bf16[4096,2048]{1,0:T(8,128)(2,1)}, bf1...) custom-call(bf16[4096,2048]{1,0:T(8,128)(2,1)} %bitcast.12, ...), custom_call_target="tpu_custom_call" | custom-call | flops 412316860416 | bytes 1073741824 | tf_op jit(solution)/shard_map/pipe_a/pallas_call | solution.py:628
  629.3 289.3 %pipe_b.1 = (bf16[4096,2048]{1,0:T(8,128)(2,1)}, bf16[4096,2048]{1,0:T(8,128)(2,1)}, bf16[4096,2048]{1,0:T(8,128)(2,1)}, bf16[4096,8192]{1,0:T(8,128)(2,1)}, f32[8192,2048]{1,0:T(8,128)}) custom-call(bf16[4096,2048]{1,0:T(8,128)(2,1)} %bitcast.14, ...), custom_call_target="tpu_custom_call", output_to_operand_aliasing={{0}: (5, {}), {1}: (6, {}), {2}: (7, {}), {3}: (8, {}), {4}... | custom-call | flops 137438953472 | bytes 536870912 | tf_op jit(solution)/shard_map/pipe_b/pallas_call | solution.py:646
  918.6 85.8 %dw2.1 = (f32[8192,2048]{1,0:T(8,128)}, bf16[4096,2048]{1,0:T(8,128)(2,1)}) custom-call(bf16[4096,8192]{1,0:T(8,128)(2,1)} %get-tuple-element.20.u.refs_4_.u_ref, bf16[4096,2048]{1,0:T(8,128)(2,1)} %get-tuple-element.26.g_ref, f32[8192,2048]{1,0:T(8,128)} %get-tuple-element.27.part_ref, bf16[4096,2048]{1,0:T(8,128)(2,1)} %get-tuple-element.28.y_ref), custom_call_target="tpu_custom_call" | custom-call | flops 68719476736 | bytes 134217728 | tf_op jit(solution)/shard_map/dw2/pallas_call | solution.py:704
  1004.4 150.8 %dw1.1 = (f32[2048,8192]{1,0:T(8,128)}, bf16[4096,2048]{1,0:T(8,128)(2,1)}) custom-call(bf16[4096,2048]{1,0:T(8,128)(2,1)} %get-tuple-element.30.h_ref, bf16[4096,8192]{1,0:T(8,128)(2,1)} %get-tuple-element.31.z_ref, bf16[4096,2048]{1,0:T(8,128)(2,1)} %get-tuple-element.32.x_ref), custom_call_target="tpu_custom_call" | custom-call | flops 137438953472 | bytes 134217728 | tf_op jit(solution)/shard_map/dw1/pallas_call | solution.py:727
  (1 shorter events, 0.0 us)

commit v3 on v2

--- a/solution.py
+++ b/solution.py
@@ -15,7 +15,8 @@
 DX_OP = 18
 Y_FIRST = 12
 Y_BLOCK = 3
-EARLY = (8, 6, 2, 0)
+DW1_EARLY = 4
+EARLY = (12, 8, 4, 0)
 VMEM_MAX = 67043328
 F32 = jnp.float32
 BF16 = jnp.bfloat16
@@ -44,14 +45,15 @@
 def _pipe_kernel(n_f, b0, n_b, *refs):
     if n_f:
         x, g, w1, w2, y, dx, hin, gin, u, dz, gp = refs[:11]
-        part = None
+        part = part1 = None
         scratch = refs[11:]
     else:
-        g, w1, w2, gp, u, _, _, _, _, _, y, dx, gin, dz, part = refs[:15]
-        x = hin = None
-        scratch = refs[15:]
+        g, w1, w2, gp, u, hin = refs[:6]
+        y, dx, gin, dz, part, part1 = refs[12:18]
+        x = None
+        scratch = refs[18:]
     fwd, recv_y, recv_dx, more = scratch[15:19]
-    _chunks(n_f, b0, n_b, x, g, w1, w2, y, dx, hin, gin, u, dz, gp, part, *scratch)
+    _chunks(n_f, b0, n_b, x, g, w1, w2, y, dx, hin, gin, u, dz, gp, part, part1, *scratch)
     s = lax.axis_index('stage')
     row, remote, wait_recv = _moves()
     n_ops = n_f + n_b
@@ -124,7 +126,7 @@
     return sum(jnp.where(s == i, c, 0) for i, c in enumerate(counts))
 
 
-def _chunks(n_f, b0, n_b, x, g, w1, w2, y, dx, hin, gin, u, dz, gp, part,
+def _chunks(n_f, b0, n_b, x, g, w1, w2, y, dx, hin, gin, u, dz, gp, part, part1,
             pin_sem, w1_sem, w2_sem, in_sem, save_sem, oue, ouo, oge, ogo, ige, igo,
             snd, snd_b, loc, recv_g, fwd, recv_y, recv_dx, more,
             w1p, w2p, w1s, w2s, acc, inb, outb, gpe, gpo, ue, uo):
@@ -134,7 +136,7 @@
     first, last = s == 0, s == 3
     n_ops = n_f + n_b
     if n_f:
-        warm = 16 - 4 * s - 4 * (s // 2) + (s // 3)
+        warm = 16 - 8 * s + 4 * (s // 2) + 5 * (s // 3)
         pairs = jnp.minimum(n_b, n_f - warm)
 
     def peer(j):
@@ -465,35 +467,52 @@
         w2_copy(3, 1).start()
         flush(dz, c, 5, 6, 7)
 
-    def half_blocks(lo, hi):
-        half = w1p.shape[1]
-
-        def g_copy(i):
-            return pltpu.make_async_copy(gin.at[pl.ds(0, half), pl.ds(i * HT, HT)], w1p.at[i], pin_sem.at[i])
-
-        def u_copy(i, slot):
-            return pltpu.make_async_copy(u.at[pl.ds(0, half), pl.ds(pl.multiple_of(i * HT, HT), HT)], w1s.at[slot], w1_sem.at[slot])
-
-        def out(i, j, p, buf, col, sem):
-            rows = pl.ds(pl.multiple_of(i * HT + j * CH, CH), CH)
-            return pltpu.make_async_copy(buf.at[p], part.at[rows, pl.ds(col * HT, HT)], sem.at[p])
+    def half_blocks(lo):
+        half, n2 = w1p.shape[1], u.shape[1] // HT
+        hi = n2 + DW1_EARLY
+
+        def cols(ref, i, n):
+            return ref.at[pl.ds(0, half), pl.ds(pl.multiple_of(i * HT, HT), n * HT)]
+
+        def loads(i, a, b):
+            slot = lax.rem(i - lo, 2)
+            return [pltpu.make_async_copy(a, w1s.at[slot], w1_sem.at[slot])] + [
+                pltpu.make_async_copy(b.at[:, pl.ds(j * HT, HT)], w1p.at[2 * slot + j], pin_sem.at[2 * slot + j]) for j in range(2)]
+
+        def start(i):
+            @pl.when(i < n2)
+            def _():
+                for copy in loads(i, cols(u, i, 1), cols(gin, 0, 2)):
+                    copy.start()
+
+            @pl.when(i >= n2)
+            def _():
+                j = (i - n2) // 2
+                for copy in loads(i, cols(hin, i - n2 - 2 * j, 1), cols(dz, 2 * j, 2)):
+                    copy.start()
+
+        def outs(i, row, p, dst, col):
+            rows = pl.ds(pl.multiple_of(row, CH), CH)
+            return [pltpu.make_async_copy(buf.at[p], dst.at[rows, pl.ds(pl.multiple_of(col + j * HT, HT), HT)], sem.at[p])
+                    for j, (buf, sem) in enumerate(((gpe, oge), (gpo, ogo)))]
+
+        def finish(p):
+            for copy in outs(lo, 0, p, part, 0):
+                copy.wait()
 
         @pl.when(lo < hi)
         def _():
-            u_copy(lo, 0).start()
-            g_copy(0).start()
-            g_copy(1).start()
-            g_copy(0).wait()
-            g_copy(1).wait()
+            start(lo)
 
             def block(i, _):
                 slot = lax.rem(i - lo, 2)
 
                 @pl.when(i + 1 < hi)
                 def _():
-                    u_copy(i + 1, 1 - slot).start()
-
-                u_copy(i, slot).wait()
+                    start(i + 1)
+
+                for copy in loads(i, cols(u, 0, 1), cols(gin, 0, 2)):
+                    copy.wait()
 
                 @pl.when(last & (i == lo + Y_BLOCK))
                 def _():
@@ -502,29 +521,37 @@
                         remote(yj, yj, fwd.at[j], recv_y.at[j], 1).start()
                         remote(yj, yj, more.at[j], recv_y.at[j], 2).start()
 
-                def strips(jj, _):
-                    @pl.when((i > lo) | (jj > 0))
+                def strip(j, _):
+                    p = lax.rem(j, 2)
+
+                    @pl.when((i > lo) | (j > 1))
                     def _():
-                        for p in range(2):
-                            out(i, 0, p, gpe, 0, oge).wait()
-                            out(i, 0, p, gpo, 1, ogo).wait()
-
-                    for p in range(2):
-                        inb[p] = w1s[slot, :, pl.ds(pl.multiple_of((2 * jj + p) * CH, CH), CH)].T
-                    for p in range(2):
-                        gpe[p] = _nn(inb[p], w1p[0])
-                        gpo[p] = _nn(inb[p], w1p[1])
-                        out(i, 2 * jj + p, p, gpe, 0, oge).start()
-                        out(i, 2 * jj + p, p, gpo, 1, ogo).start()
+                        finish(p)
+
+                    lhs = w1s[slot, :, pl.ds(pl.multiple_of(j * CH, CH), CH)]
+                    gpe[p] = _tn(lhs, w1p[2 * slot])
+                    gpo[p] = _tn(lhs, w1p[2 * slot + 1])
+                    r = i - n2
+                    j1 = r // 2
+
+                    @pl.when(r < 0)
+                    def _():
+                        for copy in outs(i, i * HT + j * CH, p, part, 0):
+                            copy.start()
+
+                    @pl.when(r >= 0)
+                    def _():
+                        for copy in outs(i, (r - 2 * j1) * HT + j * CH, p, part1, 2 * j1 * HT):
+                            copy.start()
+
                     return 0
 
-                lax.fori_loop(0, HT // CH // 2, strips, 0)
+                lax.fori_loop(0, HT // CH, strip, 0)
                 return 0
 
             lax.fori_loop(lo, hi, block, 0)
-            for p in range(2):
-                out(lo, 0, p, gpe, 0, oge).wait()
-                out(lo, 0, p, gpo, 1, ogo).wait()
+            finish(0)
+            finish(1)
 
     barrier = pltpu.get_barrier_semaphore()
     if n_f:
@@ -604,7 +631,7 @@
     free_out(n_ops)
     free_out(n_ops + 1)
     if not n_f:
-        half_blocks(_per_stage(s, EARLY), u.shape[1] // HT)
+        half_blocks(_per_stage(s, EARLY))
 
 
 def _scratch(nc, n_b, d, n_f):
@@ -632,62 +659,63 @@
         out_specs=(anyspec,) * 7,
         scratch_shapes=_scratch(nc, n_b, d, nc),
         compiler_params=pltpu.CompilerParams(collective_id=0, has_side_effects=True, vmem_limit_bytes=VMEM_MAX),
-        cost_estimate=pl.CostEstimate(flops=4 * (nc + n_b) * CH * d * h, bytes_accessed=1 << 30, transcendentals=0),
         name='pipe_a',
     )(x, g, w1, w2)
 
 
-def _second_kernel(g, w1, w2, gp, u, y, dx, gin, dz, part, b0):
+def _second_kernel(g, w1, w2, gp, u, hin, y, dx, gin, dz, part, part1, b0):
     tokens, d = g.shape
-    h = w1.shape[1]
     nc = tokens // CH
     n_b = nc - b0
     anyspec = pl.BlockSpec(memory_space=pl.ANY)
+    both = (y, dx, gin, dz, part, part1)
     return pl.pallas_call(
         functools.partial(_pipe_kernel, 0, b0, n_b),
-        out_shape=tuple(jax.ShapeDtypeStruct(a.shape, a.dtype) for a in (y, dx, gin, dz, part)),
-        in_specs=[anyspec] * 10,
-        out_specs=(anyspec,) * 5,
+        out_shape=tuple(jax.ShapeDtypeStruct(a.shape, a.dtype) for a in both),
+        in_specs=[anyspec] * 12,
+        out_specs=(anyspec,) * len(both),
         scratch_shapes=_scratch(nc, n_b, d, 0),
-        input_output_aliases={5 + i: i for i in range(5)},
+        input_output_aliases={6 + i: i for i in range(len(both))},
         compiler_params=pltpu.CompilerParams(collective_id=1, has_side_effects=True, vmem_limit_bytes=VMEM_MAX),
-        cost_estimate=pl.CostEstimate(flops=4 * n_b * CH * d * h, bytes_accessed=1 << 29, transcendentals=0),
         name='pipe_b',
-    )(g, w1, w2, gp, u, y, dx, gin, dz, part)
-
-
-def _half_blocks(lo, n, half, u, g, o):
-    def block(u_ref, g_ref, o_ref):
-        o_ref[...] = _tn(u_ref[...], g_ref[...])
-
+    )(g, w1, w2, gp, u, hin, *both)
+
+
+def _product(a_ref, b_ref, o_ref):
+    o_ref[...] = _tn(a_ref[...], b_ref[...])
+
+
+def _early_kernel(half, u, g, hin, dz, o, o1):
+    n = _per_stage(lax.axis_index('stage'), EARLY)
     d = g.shape[1]
-    pltpu.emit_pipeline(
-        block, grid=(n,),
-        in_specs=[pl.BlockSpec((half, 1024), lambda i: (0, lo + i)), pl.BlockSpec((half, d), lambda i: (0, 0))],
-        out_specs=[pl.BlockSpec((1024, d), lambda i: (lo + i, 0))])(u, g, o)
-
-
-def _early_kernel(half, u, g, o):
-    n = _per_stage(lax.axis_index('stage'), EARLY)
+    n2, nd = u.shape[1] // HT, d // HT
 
     @pl.when(n > 0)
     def _():
-        _half_blocks(0, n, half, u, g, o)
-
-
-def _early_dw2(u, gin, half):
-    tokens, h = u.shape
-    d = gin.shape[1]
+        pltpu.emit_pipeline(
+            _product, grid=(jnp.minimum(n, n2),),
+            in_specs=[pl.BlockSpec((half, HT), lambda i: (0, i)), pl.BlockSpec((half, d), lambda i: (0, 0))],
+            out_specs=[pl.BlockSpec((HT, d), lambda i: (i, 0))])(u, g, o)
+
+    @pl.when(n > n2)
+    def _():
+        pltpu.emit_pipeline(
+            _product, grid=(n - n2,),
+            in_specs=[pl.BlockSpec((half, HT), lambda i: (0, lax.rem(i, nd))), pl.BlockSpec((half, d), lambda i: (0, lax.div(i, nd)))],
+            out_specs=[pl.BlockSpec((HT, d), lambda i: (lax.rem(i, nd), lax.div(i, nd)))])(hin, dz, o1)
+
+
+def _early(u, gin, hin, dz, half):
+    h, d = u.shape[1], gin.shape[1]
     anyspec = pl.BlockSpec(memory_space=pl.ANY)
     return pl.pallas_call(
         functools.partial(_early_kernel, half),
-        in_specs=[anyspec] * 2,
-        out_specs=anyspec,
-        out_shape=jax.ShapeDtypeStruct((h, d), F32),
+        in_specs=[anyspec] * 4,
+        out_specs=(anyspec,) * 2,
+        out_shape=(jax.ShapeDtypeStruct((h, d), F32), jax.ShapeDtypeStruct((d, h), F32)),
         compiler_params=pltpu.CompilerParams(vmem_limit_bytes=VMEM_MAX),
-        cost_estimate=pl.CostEstimate(flops=half * d * h, bytes_accessed=1 << 26, transcendentals=0),
-        name='early_dw2',
-    )(u, gin)
+        name='early',
+    )(u, gin, hin, dz)
 
 
 def _dw2_kernel(u_ref, g_ref, part_ref, y_ref, o_ref, yo_ref):
@@ -698,42 +726,59 @@
 def _dw2(u, gin, part, y, half):
     tokens, h = u.shape
     d = gin.shape[1]
-    steps = h // 1024
+    steps = h // HT
     rows = pl.BlockSpec((tokens // steps, d), lambda i: (i, 0))
-    blocks = pl.BlockSpec((1024, d), lambda i: (i, 0))
+    blocks = pl.BlockSpec((HT, d), lambda i: (i, 0))
     return pl.pallas_call(
         _dw2_kernel,
         grid=(steps,),
-        in_specs=[pl.BlockSpec((half, 1024), lambda i: (1, i)),
+        in_specs=[pl.BlockSpec((half, HT), lambda i: (1, i)),
                   pl.BlockSpec((half, d), lambda i: (1, 0), pipeline_mode=pl.Buffered(1)), blocks, rows],
         out_specs=(blocks, rows),
         out_shape=(jax.ShapeDtypeStruct((h, d), F32), jax.ShapeDtypeStruct(y.shape, BF16)),
         compiler_params=pltpu.CompilerParams(vmem_limit_bytes=VMEM_MAX, dimension_semantics=('arbitrary',)),
-        cost_estimate=pl.CostEstimate(flops=tokens * d * h, bytes_accessed=1 << 27, transcendentals=0),
         name='dw2',
     )(u, gin, part, y)
 
 
-def _dw1_kernel(h_ref, z_ref, x_ref, o_ref, xo_ref):
+def _dw1_late_kernel(h_ref, z_ref, part_ref, o_ref):
+    o_ref[...] = part_ref[...] + _tn(h_ref[...], z_ref[...])
+
+
+def _dw1_kernel(h_ref, z_ref, x_ref, _, o_ref, xo_ref):
     xo_ref[...] = x_ref[...]
     o_ref[...] = _tn(h_ref[...], z_ref[...])
 
 
-def _dw1(hin, dz, dx):
+def _dw1(hin, dz, part1, dx, half):
     tokens, d = hin.shape
     h = dz.shape[1]
-    nj = h // 1024
-    rows = pl.BlockSpec((tokens // (nj * (d // 1024)), d), lambda i, j: (i * nj + j, 0))
+    nd = d // HT
+    blocks = pl.BlockSpec((HT, d), lambda i: (lax.rem(i, nd), lax.div(i, nd)))
+    out = jax.ShapeDtypeStruct((d, h), F32)
+    done = pl.pallas_call(
+        _dw1_late_kernel,
+        grid=(DW1_EARLY,),
+        in_specs=[pl.BlockSpec((half, HT), lambda i: (1, lax.rem(i, nd))), pl.BlockSpec((half, d), lambda i: (1, lax.div(i, nd))), blocks],
+        out_specs=blocks,
+        out_shape=out,
+        compiler_params=pltpu.CompilerParams(vmem_limit_bytes=VMEM_MAX, dimension_semantics=('arbitrary',)),
+        name='dw1_late',
+    )(hin, dz, part1)
+    nj = h // HT - DW1_EARLY
+    j0 = DW1_EARLY
+    rows = pl.BlockSpec((tokens // (nj * nd), d), lambda i, j: (i * nj + j, 0))
     return pl.pallas_call(
         _dw1_kernel,
-        grid=(d // 1024, nj),
-        in_specs=[pl.BlockSpec((tokens, 1024), lambda i, j: (0, i)), pl.BlockSpec((tokens, 1024), lambda i, j: (0, j)), rows],
-        out_specs=(pl.BlockSpec((1024, 1024), lambda i, j: (i, j)), rows),
-        out_shape=(jax.ShapeDtypeStruct((d, h), F32), jax.ShapeDtypeStruct(dx.shape, BF16)),
+        grid=(nd, nj),
+        in_specs=[pl.BlockSpec((tokens, HT), lambda i, j: (0, i)), pl.BlockSpec((tokens, HT), lambda i, j: (0, j0 + j)), rows,
+                  pl.BlockSpec(memory_space=pl.ANY)],
+        out_specs=(pl.BlockSpec((HT, HT), lambda i, j: (i, j0 + j)), rows),
+        out_shape=(out, jax.ShapeDtypeStruct(dx.shape, BF16)),
+        input_output_aliases={3: 0},
         compiler_params=pltpu.CompilerParams(vmem_limit_bytes=VMEM_MAX, dimension_semantics=('arbitrary', 'arbitrary')),
-        cost_estimate=pl.CostEstimate(flops=2 * tokens * d * h, bytes_accessed=1 << 27, transcendentals=0),
         name='dw1',
-    )(hin, dz, dx)
+    )(hin, dz, dx, done)
 
 
 def solution(mesh):
@@ -743,10 +788,11 @@
         b0 = tokens // CH // 2
         xt, gt = x.reshape(tokens, d), g.reshape(tokens, d)
         y, dx, hin, gin, u, dz, gp = _first_kernel(xt, gt, w1[0], w2[0], b0)
-        part = _early_dw2(u, gin, tokens // 2)
-        y, dx, gin, dz, part = _second_kernel(gt, w1[0], w2[0], gp, u, y, dx, gin, dz, part, b0)
-        dw2, y = _dw2(u, gin, part, y, tokens // 2)
-        dw1, dx = _dw1(hin, dz, dx)
+        half = tokens // 2
+        part, part1 = _early(u, gin, hin, dz, half)
+        y, dx, gin, dz, part, part1 = _second_kernel(gt, w1[0], w2[0], gp, u, hin, y, dx, gin, dz, part, part1, b0)
+        dw2, y = _dw2(u, gin, part, y, half)
+        dw1, dx = _dw1(hin, dz, part1, dx, half)
         return y.reshape(x.shape), dx.reshape(x.shape), dw1[None], dw2[None]
 
     return jax.shard_map(body, mesh=mesh,

time: 1160 us -> 1160 us (level)
    pallas_call x2 -> x3, Pallas kernels: 151 us -> 128 us  [the longest x1 81.1 us: _dw1(): pl.pallas_call(_dw1_kernel, grid=(nd, nj), in_specs=[pl.BlockSpec((tokens...]
    pallas_call x1, Pallas kernels: 289 us -> 306 us  [_second_kernel(): pl.pallas_call(functools.partial(_pipe_kernel, 0, b0, n_b), out_shape=tup...]
where the time goes in v3:
time: 1160 us; the launch traced here: 1150 us
  Pallas kernels  1150 us (99%)
    pallas_call x1, Pallas kernels, _first_kernel(): pl.pallas_call(functools.partial(_pipe_kernel, nc, 0, n_b), out_shape=(ro...  627 us
    pallas_call x1, Pallas kernels, _second_kernel(): pl.pallas_call(functools.partial(_pipe_kernel, 0, b0, n_b), out_shape=tup...  306 us
    pallas_call x1, Pallas kernels, _dw2(): pl.pallas_call(_dw2_kernel, grid=(steps,), in_specs=[pl.BlockSpec((half,...  85.8 us
    pallas_call x1, Pallas kernels, _dw1(): pl.pallas_call(_dw1_kernel, grid=(nd, nj), in_specs=[pl.BlockSpec((tokens...  81.1 us
    pallas_call x1, Pallas kernels, _dw1(): pl.pallas_call(_dw1_late_kernel, grid=(DW1_EARLY,), in_specs=[pl.BlockSpe...  47.3 us

profile of v3, /device:TPU:7, one launch (start us, length us, event | category | flops | bytes accessed | tf_op | source)
XLA Modules:
  0.0 1148.5 jit_solution(13575583191130363378)
XLA Ops:
  0.6 627.0 %pipe_a.1 = (bf16[4096,2048]{1,0:T(8,128)(2,1)}, bf16[4096,2048]{1,0:T(8,128)(2,1)}, bf16[4096,2048]{1,0:T(8,128)(2,1)}, bf16[4096,2048]{1,0:T(8,128)(2,1)}, bf1...) custom-call(bf16[4096,2048]{1,0:T(8,128)(2,1)} %bitcast.14, ...), custom_call_target="tpu_custom_call" | custom-call | tf_op jit(solution)/shard_map/pipe_a/pallas_call | solution.py:655
  627.6 306.2 %pipe_b.1 = (bf16[4096,2048]{1,0:T(8,128)(2,1)}, bf16[4096,2048]{1,0:T(8,128)(2,1)}, bf16[4096,2048]{1,0:T(8,128)(2,1)}, bf16[4096,8192]{1,0:T(8,128)(2,1)}, f32[8192,2048]{1,0:T(8,128)}, /*index=5*/f32[2048,8192]{1,0:T(8,128)}) custom-call(bf16[4096,2048]{1,0:T(8,128)(2,1)} %bitcast.13, ...), custom_call_target="tpu_custom_call", output_to_operand_aliasing={{0}: (6, {}), {1}: (7, {}), {2}: (8, {}), {3}: (9, {}), {4}... | custom-call | tf_op jit(solution)/shard_map/pipe_b/pallas_call | solution.py:672
  933.8 85.8 %dw2.1 = (f32[8192,2048]{1,0:T(8,128)}, bf16[4096,2048]{1,0:T(8,128)(2,1)}) custom-call(bf16[4096,8192]{1,0:T(8,128)(2,1)} %get-tuple-element.23.u.refs_4_.u_ref, bf16[4096,2048]{1,0:T(8,128)(2,1)} %get-tuple-element.32.g_ref, f32[8192,2048]{1,0:T(8,128)} %get-tuple-element.33.part_ref, bf16[4096,2048]{1,0:T(8,128)(2,1)} %get-tuple-element.34.y_ref), custom_call_target="tpu_custom_call" | custom-call | tf_op jit(solution)/shard_map/dw2/pallas_call | solution.py:732
  1019.7 47.3 %dw1_late.1._ = f32[2048,8192]{1,0:T(8,128)} custom-call(bf16[4096,2048]{1,0:T(8,128)(2,1)} %get-tuple-element.25.hin.refs_5_.h_ref, bf16[4096,8192]{1,0:T(8,128)(2,1)} %get-tuple-element.36.z_ref, f32[2048,8192]{1,0:T(8,128)} %get-tuple-element.38.part_ref), custom_call_target="tpu_custom_call" | custom-call | tf_op jit(solution)/shard_map/dw1_late/pallas_call | solution.py:759
  1067.0 81.1 %dw1.1 = (f32[2048,8192]{1,0:T(8,128)}, bf16[4096,2048]{1,0:T(8,128)(2,1)}) custom-call(bf16[4096,2048]{1,0:T(8,128)(2,1)} %get-tuple-element.25.hin.refs_5_.h_ref, bf16[4096,8192]{1,0:T(8,128)(2,1)} %get-tuple-element.36.z_ref, bf16[4096,2048]{1,0:T(8,128)(2,1)} %get-tuple-element.37.x_ref, f32[2048,8192]{1,0:T(8,128)} %dw1_late.1._), custom_call_target="tpu_custom_call", output_to_operand_aliasing={{0}: (3, {})} | custom-call | tf_op jit(solution)/shard_map/dw1/pallas_call | solution.py:771
  (1 shorter events, 0.0 us)

commit v4 on v3

--- a/solution.py
+++ b/solution.py
@@ -16,7 +16,7 @@
 Y_FIRST = 12
 Y_BLOCK = 3
 DW1_EARLY = 4
-EARLY = (12, 8, 4, 0)
+EARLY = (11, 8, 4, 0)
 VMEM_MAX = 67043328
 F32 = jnp.float32
 BF16 = jnp.bfloat16
@@ -136,7 +136,7 @@
     first, last = s == 0, s == 3
     n_ops = n_f + n_b
     if n_f:
-        warm = 16 - 8 * s + 4 * (s // 2) + 5 * (s // 3)
+        warm = 16 - 4 * s - 4 * (s // 2) + (s // 3)
         pairs = jnp.minimum(n_b, n_f - warm)
 
     def peer(j):

time: 1160 us -> 1150 us (level)
  no operation moved by 1% of the time
where the time goes in v4:
time: 1150 us; the launch traced here: 1140 us
  Pallas kernels  1140 us (99%)
    pallas_call x1, Pallas kernels, _first_kernel(): pl.pallas_call(functools.partial(_pipe_kernel, nc, 0, n_b), out_shape=(ro...  620 us
    pallas_call x1, Pallas kernels, _second_kernel(): pl.pallas_call(functools.partial(_pipe_kernel, 0, b0, n_b), out_shape=tup...  303 us
    pallas_call x1, Pallas kernels, _dw2(): pl.pallas_call(_dw2_kernel, grid=(steps,), in_specs=[pl.BlockSpec((half,...  85.8 us
    pallas_call x1, Pallas kernels, _dw1(): pl.pallas_call(_dw1_kernel, grid=(nd, nj), in_specs=[pl.BlockSpec((tokens...  81.1 us
    pallas_call x1, Pallas kernels, _dw1(): pl.pallas_call(_dw1_late_kernel, grid=(DW1_EARLY,), in_specs=[pl.BlockSpe...  47.3 us

profile of v4, /device:TPU:7, one launch (start us, length us, event | category | flops | bytes accessed | tf_op | source)
XLA Modules:
  0.0 1138.1 jit_solution(7765514778305857396)
XLA Ops:
  0.6 619.6 %pipe_a.1 = (bf16[4096,2048]{1,0:T(8,128)(2,1)}, bf16[4096,2048]{1,0:T(8,128)(2,1)}, bf16[4096,2048]{1,0:T(8,128)(2,1)}, bf16[4096,2048]{1,0:T(8,128)(2,1)}, bf1...) custom-call(bf16[4096,2048]{1,0:T(8,128)(2,1)} %bitcast.14, ...), custom_call_target="tpu_custom_call" | custom-call | tf_op jit(solution)/shard_map/pipe_a/pallas_call | solution.py:655
  620.2 303.2 %pipe_b.1 = (bf16[4096,2048]{1,0:T(8,128)(2,1)}, bf16[4096,2048]{1,0:T(8,128)(2,1)}, bf16[4096,2048]{1,0:T(8,128)(2,1)}, bf16[4096,8192]{1,0:T(8,128)(2,1)}, f32[8192,2048]{1,0:T(8,128)}, /*index=5*/f32[2048,8192]{1,0:T(8,128)}) custom-call(bf16[4096,2048]{1,0:T(8,128)(2,1)} %bitcast.13, ...), custom_call_target="tpu_custom_call", output_to_operand_aliasing={{0}: (6, {}), {1}: (7, {}), {2}: (8, {}), {3}: (9, {}), {4}... | custom-call | tf_op jit(solution)/shard_map/pipe_b/pallas_call | solution.py:672
  923.4 85.8 %dw2.1 = (f32[8192,2048]{1,0:T(8,128)}, bf16[4096,2048]{1,0:T(8,128)(2,1)}) custom-call(bf16[4096,8192]{1,0:T(8,128)(2,1)} %get-tuple-element.23.u.refs_4_.u_ref, bf16[4096,2048]{1,0:T(8,128)(2,1)} %get-tuple-element.32.g_ref, f32[8192,2048]{1,0:T(8,128)} %get-tuple-element.33.part_ref, bf16[4096,2048]{1,0:T(8,128)(2,1)} %get-tuple-element.34.y_ref), custom_call_target="tpu_custom_call" | custom-call | tf_op jit(solution)/shard_map/dw2/pallas_call | solution.py:732
  1009.3 47.3 %dw1_late.1._ = f32[2048,8192]{1,0:T(8,128)} custom-call(bf16[4096,2048]{1,0:T(8,128)(2,1)} %get-tuple-element.25.hin.refs_5_.h_ref, bf16[4096,8192]{1,0:T(8,128)(2,1)} %get-tuple-element.36.z_ref, f32[2048,8192]{1,0:T(8,128)} %get-tuple-element.38.part_ref), custom_call_target="tpu_custom_call" | custom-call | tf_op jit(solution)/shard_map/dw1_late/pallas_call | solution.py:759
  1056.6 81.1 %dw1.1 = (f32[2048,8192]{1,0:T(8,128)}, bf16[4096,2048]{1,0:T(8,128)(2,1)}) custom-call(bf16[4096,2048]{1,0:T(8,128)(2,1)} %get-tuple-element.25.hin.refs_5_.h_ref, bf16[4096,8192]{1,0:T(8,128)(2,1)} %get-tuple-element.36.z_ref, bf16[4096,2048]{1,0:T(8,128)(2,1)} %get-tuple-element.37.x_ref, f32[2048,8192]{1,0:T(8,128)} %dw1_late.1._), custom_call_target="tpu_custom_call", output_to_operand_aliasing={{0}: (3, {})} | custom-call | tf_op jit(solution)/shard_map/dw1/pallas_call | solution.py:771
  (1 shorter events, 0.0 us)
